TPU v7x, 32 devices: a whole 2x2x4 slice. The times are simulated.
32 devices in a mesh: corpus: 8 (over z, y), neur: 4 (over x, core).
Axes of the slice: x: 2, y: 2, z: 4, core: 2. Of those that a mesh axis runs over, the one named last changes fastest.
Arguments:
- resid: bfloat16 [32768, 4096], P(('corpus', 'neur')), may hold values from -140 to 140
- norm_gain: float32 [4096], replicated, may hold values from 0.1 to 1.9
- w_gate: bfloat16 [4096, 6144], P(None, 'neur'), may hold values from -0.09375 to 0.09375
- w_up: bfloat16 [4096, 6144], P(None, 'neur'), may hold values from -0.09375 to 0.09375
- hit_neuron: int32 [2048], P(('corpus', 'neur')), may hold values from 0 to 6143, as said below
- hit_start: int32 [2048], P(('corpus', 'neur')), may hold values from 0 to 32736, as said below
- hit_mask: int32 [2048, 32], P(('corpus', 'neur')), may hold values from 0 to 1, as said below
Outputs:
- profile: float32 [2048, 32], P(('corpus', 'neur'))
- coact: float32 [2048, 1536], P(('corpus', 'neur'))
Inputs may be any that keep to these rules, and one draw needn't show every extreme that they name: `hit_start`: every window of 32 tokens lies inside one aligned block of 1024 corpus tokens. Among the hits of one device (blocks of 64 hits) at most 4 window lies in one such block; this bound is reached by every device in every draw. `hit_neuron`: the hits of block b of 64 hits (blocks in the order corpus+neur) name neurons of block b % 4 of 6144 // 4 neurons. `hit_mask`: the ones of each row form one run that contains positions 15 and 16.
All inputs are finite; a program needn't handle non-finite values.
Results may differ from a plain program's by a relative error of at most 0.0042.
Values may be sent and summed in bfloat16 or wider, within the bound.
No kernel may reach another device: no remote copies, remote signals or barrier semaphores. Data moves between devices by JAX's collectives and lax.ppermute only.
A program may use at most 320 MiB of HBM per device.

v0:
```python
import jax
import jax.numpy as jnp
from jax import lax
from jax.sharding import PartitionSpec as P

EPS = 1e-05


def normed_acts(rows, norm_gain, w_gate, w_up):
    values = rows.astype(jnp.float32)
    power = jnp.mean(values * values, axis=-1, keepdims=True)
    normed = (values * lax.rsqrt(power + EPS) * norm_gain).astype(jnp.bfloat16)
    gate = jnp.dot(normed, w_gate, preferred_element_type=jnp.float32)
    upward = jnp.dot(normed, w_up, preferred_element_type=jnp.float32)
    return jax.nn.silu(gate) * upward


def slot_plan(starts, block_rows, owners, slots):
    owner_of = starts // block_rows
    position = jnp.arange(starts.shape[0], dtype=jnp.int32)
    earlier = (owner_of[:, None] == owner_of[None, :]) & (position[None, :] < position[:, None])
    rank_of = jnp.sum(earlier.astype(jnp.int32), axis=1)
    target = owner_of * slots + rank_of
    placed = target[:, None] == jnp.arange(owners * slots, dtype=jnp.int32)[None, :]
    local_start = starts - owner_of * block_rows
    offsets = jnp.sum(jnp.where(placed, local_start[:, None], 0), axis=0)
    return (target, offsets.reshape(owners, slots))


def cut_windows(resid, offsets, width):
    steps = jnp.arange(width, dtype=jnp.int32)
    row_ids = offsets[..., None] + steps
    taken = jnp.take(resid, row_ids.reshape(-1), axis=0)
    return taken.reshape(offsets.shape + (width, resid.shape[1]))


def per_device(resid, norm_gain, w_gate, w_up, hit_neuron, hit_start, hit_mask):
    width = hit_mask.shape[1]
    block_rows = resid.shape[0]
    model_width = resid.shape[1]
    corpus_count = lax.axis_size("corpus")
    neuron_count = lax.axis_size("neur")
    devices = corpus_count * neuron_count
    own_hits = hit_start.shape[0]
    local_width = w_gate.shape[1]
    slots = max(1, 2 * own_hits // devices)
    target, offsets = slot_plan(hit_start, block_rows, devices, slots)
    fetched = lax.all_to_all(
        cut_windows(
            resid,
            lax.all_to_all(offsets, ("corpus", "neur"), split_axis=0, concat_axis=0, tiled=True),
            width,
        ),
        ("corpus", "neur"),
        split_axis=0,
        concat_axis=0,
        tiled=True,
    )
    rows = jnp.take(fetched.reshape(devices * slots, width, model_width), target, axis=0)
    acts = normed_acts(rows.reshape(-1, model_width), norm_gain, w_gate, w_up)
    acts = acts.reshape(own_hits, width, local_width)
    live = hit_mask > 0
    coact = jnp.max(jnp.where(live[:, :, None], acts, -jnp.inf), axis=1)
    member = lax.axis_index("neur")
    local_neuron = hit_neuron - member * local_width
    chosen = jnp.arange(local_width, dtype=jnp.int32)[None, None, :] == local_neuron[:, None, None]
    profile = jnp.sum(jnp.where(chosen, acts, 0.0), axis=-1) * hit_mask.astype(jnp.float32)
    return (profile, coact)


def solution(mesh):
    placed = (
        P(("corpus", "neur"), None),
        P(),
        P(None, "neur"),
        P(None, "neur"),
        P(("corpus", "neur")),
        P(("corpus", "neur")),
        P(("corpus", "neur"), None),
    )
    return jax.shard_map(
        per_device,
        mesh=mesh,
        in_specs=placed,
        out_specs=(P(("corpus", "neur"), None), P(("corpus", "neur"), None)),
        check_vma=False,
    )
```

profile of v0, /device:TPU:0, one launch (start us, length us, event | category | flops | bytes accessed | tf_op | source)
XLA Modules:
  0.0 962.4 jit_solution(2120811792964550653)
XLA Ops:
  0.6 0.7 multiply_subtract_fusion
  1.3 0.2 convert_reduce_fusion
  1.5 0.1 select_reduce_fusion.2
  1.6 0.1 all_to_all.9
  1.7 14.3 %all_to_all.14 = s32[32,1,4]{2,1,0:T(1,128)S(1)} all-to-all(s32[32,1,4]{2,1,0:T(1,128)S(1)} %bitcast.20), channel_id=1, replica_groups=mesh['corpus'=8,'neur'=4] {'corpus','neur'}, dimensions={0} | all-to-all | bytes 1024 | tf_op jit(solution)/shard_map/all_to_all | solution.py:51
  16.0 0.1 iota_add_fusion
  16.1 0.1 compare_and_fusion
  16.2 0.1 add.88
  16.4 60.3 %gather_fusion = bf16[4096,4096]{1,0:T(8,128)(2,1)} fusion(bf16[1024,4096]{1,0:T(8,128)(2,1)} %param.7, s32[4096]{0:T(1024)S(1)} %broadcast_clamp_fusion), kind=kCustom, calls=%fused_computation | custom fusion | bytes 67125248 | tf_op jit(solution)/shard_map/jit(_take)/gather | solution.py:33
  76.7 23.1 %broadcast_select_fusion = bf16[32,4,32,4096]{3,2,1,0:T(8,128)(2,1)} fusion(bf16[32,4,32,4096]{3,2,1,0:T(8,128)(2,1)} %bitcast.17, pred[32,4,32]{2,1,0:T(4,128)(4,1)S(1)} %compare_and_fusion), kind=kLoop, calls=%fused_computation.4 | loop fusion | flops 16777216 | bytes 67112960 | tf_op jit(solution)/shard_map/jit(_take)/select_n | solution.py:33
  99.8 4.6 all-to-all-start.1
  104.4 0.1 broadcast_in_dim.84
  104.5 0.1 broadcast_in_dim.85
  104.6 0.1 copy.26
  104.7 0.1 copy.27
  104.9 0.1 iota_compare_fusion
  105.0 748.6 %all-to-all-done.1 = bf16[32,4,32,4096]{3,2,1,0:T(8,128)(2,1)} async-done(((bf16[32,4,32,4096]{3,2,1,0:T(8,128)(2,1)}), bf16[32,4,32,4096]{3,2,1,0:T(8,128)(2,1)}, u32[]{:S(2)}, u32[]{:S(2)}) %all-to-all-start.1) | async-done | bytes 33554464 | tf_op jit(solution)/shard_map/all_to_all | solution.py:48
  853.6 11.8 %gather_fusion.1 = bf16[64,32,4096]{2,1,0:T(8,128)(2,1)} fusion(bf16[128,32,4096]{2,1,0:T(8,128)(2,1)} %bitcast.5, s32[1024]{0:T(1024)S(1)} %pad_clamp_fusion), kind=kCustom, calls=%fused_computation.1 | custom fusion | bytes 33554688 | tf_op jit(solution)/shard_map/jit(_take)/gather | solution.py:59
  865.4 7.9 multiply_reduce_fusion
  873.4 11.7 %multiply_convert_fusion = bf16[2048,4096]{1,0:T(8,128)(2,1)S(1)} fusion(bf16[64,32,4096]{2,1,0:T(8,128)(2,1)} %gather_fusion.1, f32[4096]{0:T(1024)S(1)} %copy-done.1, f32[2048]{0:T(1024)S(1)} %rsqrt.12, pred[2048]{0:T(1024)(128)(4,1)S(1)} %broadcast_in_dim.85), kind=kLoop, calls=%fused_computation.2 | loop fusion | flops 41943040 | bytes 33581056 | tf_op jit(solution)/shard_map/convert_element_type | solution.py:12
  885.1 31.5 %fusion.1 = f32[2048,1536]{1,0:T(8,128)} fusion(bf16[2048,4096]{1,0:T(8,128)(2,1)S(1)} %multiply_convert_fusion, bf16[4096,1536]{1,0:T(8,128)(2,1)} %param.9), kind=kOutput, calls=%fused_computation.33 | convolution fusion | flops 25769803776 | bytes 41943040 | tf_op jit(solution)/shard_map/dot_general | solution.py:13
  916.6 37.3 %select_reduce_fusion.1 = (f32[2048]{0:T(1024)S(1)}, f32[2048,1536]{1,0:T(8,128)}) fusion(pred[64,1536]{1,0:T(8,128)(4,1)S(1)} %iota_compare_fusion, bf16[2048,4096]{1,0:T(8,128)(2,1)S(1)} %multiply_convert_fusion, bf16[4096,1536]{1,0:T(8,128)(2,1)} %param.10, f32[2048,1536]{1,0:T(8,128)} %fusion.1), kind=kOutput, calls=%fused_computation.7 | convolution fusion | flops 25791821824 | bytes 54632448 | tf_op jit(solution)/shard_map/dot_general | solution.py:14
  954.0 0.7 copy.28
  954.7 7.7 select_reduce_fusion
  (17 shorter events, 0.2 us)
Async XLA Ops:
  99.8 4.8 copy-start
  99.8 5.0 copy-start.2
  99.8 753.8 %all-to-all-start.1 = ((bf16[32,4,32,4096]{3,2,1,0:T(8,128)(2,1)}), bf16[32,4,32,4096]{3,2,1,0:T(8,128)(2,1)}, u32[]{:S(2)}, u32[]{:S(2)}) async-start(bf16[32,4,32,4096]{3,2,1,0:T(8,128)(2,1)} %broadcast_select_fusion), calls=%async_computation.1 | async-start | bytes 67108864 | tf_op jit(solution)/shard_map/all_to_all | solution.py:48
  865.4 8.0 copy-start.1
where the time goes:
time: 963 us; the launch traced here: 962 us
  waiting for transfers between devices  749 us (78%)
  local copies, waits for them, and re-layouts  73.5 us (8%)
  matrix products  68.8 us (7%)
  other arithmetic  51.8 us (5%)
  blocking collectives  14.3 us (1%)
    all_to_all x1, waiting for transfers between devices, per_device(): lax.all_to_all(cut_windows(resid, lax.all_to_all(offsets, ('corpus', 'neu...  749 us
    gather x1, local copies, waits for them, and re-layouts, cut_windows(): taken = jnp.take(resid, row_ids.reshape(-1), axis=0)  60.3 us
    dot_general x1, matrix products, normed_acts(): upward = jnp.dot(normed, w_up, preferred_element_type=jnp.float32)  37.3 us
    dot_general x1, matrix products, normed_acts(): gate = jnp.dot(normed, w_gate, preferred_element_type=jnp.float32)  31.5 us
    select_n x2, other arithmetic, cut_windows(): taken = jnp.take(resid, row_ids.reshape(-1), axis=0)  23.1 us
  transfers between devices with their start and end apart: 1, of which 1 were waited for; matrix products, arithmetic and copies ran while one was open for 0% of the time, Pallas kernels for 0%

commit v1 on v0

v1 whole, which is shorter than its diff:
```python
import functools

import jax
import jax.numpy as jnp
from jax import lax
from jax.experimental import pallas as pl
from jax.experimental.pallas import tpu as pltpu
from jax.sharding import PartitionSpec as P


EPS = 1e-05
GRAN = 8
LANES = 128
SENT = 4
FIELDS = 5
PIECES = (3, 4, 4, 3, 1, 1)
STRIP = 128
ROOM = 13 * 1024 * 1024
ROOM_STREAMED = 46 * 1024 * 1024


def norm_kernel(rows, gain, *outs, starts, counts):
    step = pl.program_id(0)
    strip = 16
    scale = gain[...].reshape(1, -1)

    for out, start, count in zip(outs, starts, counts):

        @pl.when((step >= start) & (step < start + count))
        def _():
            def one(i, carry):
                at = pl.multiple_of(i * strip, strip)
                values = rows[pl.ds(at, strip), :].astype(jnp.float32)
                power = jnp.mean(values * values, axis=-1, keepdims=True)
                scaled = values * lax.rsqrt(power + EPS) * scale
                out[pl.ds(at, strip), :] = scaled.astype(jnp.bfloat16)
                return carry

            lax.fori_loop(0, rows.shape[0] // strip, one, 0, unroll=2)


def norm_pieces(resid, gain, first_row, sizes, part):
    model_width = resid.shape[1]
    counts = [size // part for size in sizes]
    starts = [sum(counts[:i]) for i in range(len(sizes))]
    skip = first_row // part

    def piece_spec(start, count):
        return pl.BlockSpec((part, model_width), lambda j: (jnp.clip(j - start, 0, count - 1), 0))

    return pl.pallas_call(
        functools.partial(norm_kernel, starts=starts, counts=counts),
        grid=(sum(counts),),
        in_specs=[
            pl.BlockSpec((part, model_width), lambda j: (j + skip, 0)),
            pl.BlockSpec((model_width,), lambda j: (0,)),
        ],
        out_specs=[piece_spec(start, count) for start, count in zip(starts, counts)],
        out_shape=[jax.ShapeDtypeStruct((size, model_width), jnp.bfloat16) for size in sizes],
        compiler_params=pltpu.CompilerParams(
            dimension_semantics=("arbitrary",), vmem_limit_bytes=16 * 1024 * 1024
        ),
        name="norm_rows",
    )(resid, gain)


def block_kernel(table, order, bounds, *rest, spans, slots_rel, fresh, streamed):
    rows, rest = rest[:2 * len(spans)], rest[2 * len(spans):]
    w_gate, w_up, *rest = rest
    if fresh:
        before = None
        msg, acts, stack, sem = rest
    else:
        before, msg, acts, stack, sem = rest
    local_width = acts.shape[1]
    tile = w_gate.shape[1] if streamed else tile_of(local_width)
    slot_count = msg.shape[0]
    reach = acts.shape[0] - stack.shape[0]
    marks = bounds.shape[0] // 2
    listed = order.shape[0] // 2
    first_mark, last_mark = spans[0][0], spans[-1][0] + 1
    bases = [bounds[half * marks + first_mark] for half in range(2)]
    ends = [bounds[half * marks + last_mark] for half in range(2)]
    shifts = [0 - bases[0], ends[0] - bases[0] - bases[1]]
    total = ends[1] + shifts[1]

    def granule_copy(i, at, to):
        return pltpu.make_async_copy(
            rows[i].at[pl.ds(pl.multiple_of(at * GRAN, GRAN), GRAN), :],
            stack.at[pl.ds(pl.multiple_of(to * GRAN, GRAN), GRAN), :],
            sem,
        )

    def load_rows():
        for half in range(2):
            for i, (mark, first) in enumerate(spans):

                def one(rank, carry):
                    at = order[half * listed + rank] - first
                    granule_copy(half * len(spans) + i, at, rank + shifts[half]).start()
                    return carry

                lax.fori_loop(bounds[half * marks + mark], bounds[half * marks + mark + 1], one, 0)
        if fresh:
            msg[...] = jnp.full(msg.shape, -jnp.inf, jnp.float32)
        else:
            msg[...] = before[...]

        def settle(g, carry):
            granule_copy(0, 0, 0).wait()
            return carry

        lax.fori_loop(0, total, settle, 0)

    def one_tile(gate_tile, up_tile, at):
        columns = pl.ds(pl.multiple_of(at, tile), tile)

        def part(m, carry):
            span = pl.ds(pl.multiple_of(m * STRIP, STRIP), STRIP)
            gate = jnp.dot(stack[span, :], gate_tile(), preferred_element_type=jnp.float32)
            upward = jnp.dot(stack[span, :], up_tile(), preferred_element_type=jnp.float32)
            acts[span, columns] = gate / (1.0 + jnp.exp(-gate)) * upward
            return carry

        lax.fori_loop(0, (total * GRAN + STRIP - 1) // STRIP, part, 0)

    def read_hits():
        local = lax.broadcasted_iota(jnp.int32, (reach, 1), 0)
        lane = lax.broadcasted_iota(jnp.int32, (reach, LANES), 1)
        local_full = lax.broadcasted_iota(jnp.int32, (reach, LANES), 0)

        def one_slot(slot, carry):
            rank_low = table[slot * FIELDS]
            rank_high = table[slot * FIELDS + 1]
            second = (slot // slots_rel) % 2 == 1
            base = jnp.where(second, bases[1], bases[0])
            end = jnp.where(second, ends[1], ends[0])

            @pl.when((rank_high >= base) & (rank_low < end))
            def _():
                low = table[slot * FIELDS + 2]
                high = table[slot * FIELDS + 3]
                neuron = table[slot * FIELDS + 4]
                rank = jnp.maximum(rank_low, base)
                here = (jnp.minimum(rank_high + 1, end) - rank) * GRAN
                past = (rank - rank_low) * GRAN + low // GRAN * GRAN
                top = pl.multiple_of((rank + jnp.where(second, shifts[1], shifts[0])) * GRAN, GRAN)
                live = (local >= low - past) & (local <= high - past) & (local < here)
                best = jnp.max(jnp.where(live, acts[pl.ds(top, reach), :], -jnp.inf), axis=0, keepdims=True)
                column = pl.multiple_of(neuron // LANES * LANES, LANES)
                near = acts[pl.ds(top, reach), pl.ds(column, LANES)]
                picked = jnp.sum(jnp.where(lane == neuron % LANES, near, 0.0), axis=1, keepdims=True)
                mine = (lane == local_full + past) & (local_full < here)
                placed = jnp.max(jnp.where(mine, picked, -jnp.inf), axis=0, keepdims=True)
                found = jnp.concatenate([best, placed], axis=1)
                msg[pl.ds(slot, 1), :] = jnp.maximum(msg[pl.ds(slot, 1), :], found)

            return carry

        lax.fori_loop(0, slot_count, one_slot, 0)

    if streamed:
        step = pl.program_id(0)
        pl.when(step == 0)(load_rows)
        one_tile(lambda: w_gate[...], lambda: w_up[...], step * tile)
        pl.when(step == pl.num_programs(0) - 1)(read_hits)
    else:
        load_rows()

        def body(j, carry):
            columns = pl.ds(pl.multiple_of(j * tile, tile), tile)
            one_tile(lambda: w_gate[:, columns], lambda: w_up[:, columns], j * tile)
            return carry

        lax.fori_loop(0, local_width // tile, body, 0)
        read_hits()


def tile_of(local_width):
    return 256 if local_width % 256 == 0 else local_width


def run_block(plan, pieces, w_gate, w_up, before, width, slots_rel, streamed):
    table, order, bounds = plan
    model_width, local_width = w_gate.shape
    slot_count = table.shape[0] // FIELDS
    spans = [(mark, first // GRAN) for mark, first, _, _ in pieces]
    rows = [p[2] for p in pieces] + [p[3] for p in pieces]
    row_count = sum(r.shape[0] for r in rows)
    reach = (width + 2 * GRAN - 2) // GRAN * GRAN
    fresh = before is None
    msg_shape = (slot_count, local_width + LANES)
    if streamed:
        tile = tile_of(local_width)
        grid = (local_width // tile,)
        weight = pl.BlockSpec((model_width, tile), lambda j: (0, j))
        whole = pl.BlockSpec(msg_shape, lambda j: (0, 0))
    else:
        grid = ()
        weight = whole = pl.BlockSpec(memory_space=pltpu.VMEM)
    in_specs = [pl.BlockSpec(memory_space=pltpu.SMEM)] * 3
    in_specs += [pl.BlockSpec(memory_space=pltpu.HBM)] * len(rows)
    in_specs += [weight, weight]
    operands = [table, order, bounds, *rows, w_gate, w_up]
    aliases = {}
    if not fresh:
        in_specs.append(whole)
        operands.append(before)
        aliases = {len(operands) - 1: 0}
    return pl.pallas_call(
        functools.partial(
            block_kernel,
            spans=spans,
            slots_rel=slots_rel,
            fresh=fresh,
            streamed=streamed,
        ),
        grid=grid,
        in_specs=in_specs,
        out_specs=whole,
        out_shape=jax.ShapeDtypeStruct(msg_shape, jnp.float32),
        scratch_shapes=[
            pltpu.VMEM((row_count + reach, local_width), jnp.float32),
            pltpu.VMEM((row_count, model_width), jnp.bfloat16),
            pltpu.SemaphoreType.DMA,
        ],
        input_output_aliases=aliases,
        compiler_params=pltpu.CompilerParams(vmem_limit_bytes=ROOM_STREAMED if streamed else ROOM),
        cost_estimate=pl.CostEstimate(
            flops=2 * row_count * model_width * local_width,
            transcendentals=row_count * local_width,
            bytes_accessed=4 * model_width * local_width,
        ),
        name="block_acts",
    )(*operands)


def collect_kernel(where, shift, mask, *rest, phases, rows_each, local_width):
    parts = rest[:phases]
    profile, coact, whole = rest[phases:]
    for p in range(phases):
        whole[p * rows_each:(p + 1) * rows_each, :] = parts[p][...].astype(jnp.float32)
    width = profile.shape[1]

    def one(hit, carry):
        at = where[hit]
        row = whole[pl.ds(at, 1), :]
        coact[pl.ds(hit, 1), :] = row[:, :local_width]
        moved = pltpu.roll(jnp.broadcast_to(row[:, local_width:], (GRAN, LANES)), LANES - shift[hit], 1)
        profile[pl.ds(hit, 1), :] = jnp.where(mask[pl.ds(hit, 1), :] > 0, moved[:1, :width], 0.0)
        return carry

    lax.fori_loop(0, profile.shape[0], one, 0, unroll=8)


def collect(where, shift, mask, parts, local_width):
    own_hits, width = mask.shape
    rows_each = parts[0].shape[0]
    vmem = pl.BlockSpec(memory_space=pltpu.VMEM)
    smem = pl.BlockSpec(memory_space=pltpu.SMEM)
    return pl.pallas_call(
        functools.partial(collect_kernel, phases=len(parts), rows_each=rows_each, local_width=local_width),
        in_specs=[smem, smem, vmem] + [vmem] * len(parts),
        out_specs=(vmem, vmem),
        out_shape=(
            jax.ShapeDtypeStruct((own_hits, width), jnp.float32),
            jax.ShapeDtypeStruct((own_hits, local_width), jnp.float32),
        ),
        scratch_shapes=[pltpu.VMEM((len(parts) * rows_each, local_width + LANES), jnp.float32)],
        compiler_params=pltpu.CompilerParams(vmem_limit_bytes=16 * 1024 * 1024),
        name="collect_hits",
    )(where, shift, mask, *parts)


def in_hbm(x):
    return pltpu.with_memory_space_constraint(x, pltpu.HBM)


def per_device(resid, norm_gain, w_gate, w_up, hit_neuron, hit_start, hit_mask):
    resid = in_hbm(resid)
    width = hit_mask.shape[1]
    block_rows, _ = resid.shape
    groups = lax.axis_size("corpus")
    columns = lax.axis_size("neur")
    devices = groups * columns
    own_hits = hit_start.shape[0]
    local_width = w_gate.shape[1]
    slots = max(1, 2 * own_hits // devices)
    member = lax.axis_index("neur")
    chips = columns // 2
    gain = in_hbm(norm_gain)

    unit = block_rows // 16
    sizes = [unit * n for n in PIECES]
    firsts = [sum(sizes[:i]) for i in range(len(sizes))]
    own = norm_pieces(resid, gain, 0, sizes[:1], unit)
    own = own + norm_pieces(resid, gain, sizes[0], sizes[1:], unit)
    own = [in_hbm(piece) for piece in own]
    swap = [(i, i ^ 1) for i in range(columns)]
    far = []
    for s in range(1, chips):
        ring = [(i, (i + 2 * s) % columns) for i in range(columns)]
        pieces = []
        for piece in own:
            pieces.append(in_hbm(lax.ppermute(piece, "neur", ring)))
        far.append(pieces)
    sibling = [in_hbm(lax.ppermute(piece, "neur", swap)) for piece in own]

    owner = hit_start // block_rows
    owner_group = owner // columns
    owner_column = owner % columns
    phase = (member // 2 - owner_column // 2) % chips
    rel = (owner_column % 2) ^ (member % 2)
    position = jnp.arange(own_hits, dtype=jnp.int32)
    earlier = (owner[:, None] == owner[None, :]) & (position[None, :] < position[:, None])
    rank = jnp.sum(earlier.astype(jnp.int32), axis=1)
    target = ((owner_group * chips + phase) * 2 + rel) * slots + rank
    local_start = hit_start - owner * block_rows
    shift = local_start % GRAN
    live = hit_mask > 0
    steps = jnp.arange(width, dtype=jnp.int32)[None, :]
    low = jnp.min(jnp.where(live, steps, width), axis=1) + shift
    high = jnp.max(jnp.where(live, steps, -1), axis=1) + shift
    fields = jnp.stack([local_start + 1, low, high, hit_neuron - member * local_width], axis=1)
    placed = target[:, None] == jnp.arange(devices * slots, dtype=jnp.int32)[None, :]
    sheet = jnp.sum(jnp.where(placed[:, :, None], fields[:, None, :], 0), axis=0)
    sheet = lax.all_to_all(sheet.reshape(groups, -1), "corpus", split_axis=0, concat_axis=0, tiled=True)
    sheet = sheet.reshape(groups, chips * 2 * slots, SENT)
    sheet = sheet - jnp.array([1, 0, 0, 0], jnp.int32)

    def send_back(msg):
        msg = msg.astype(jnp.bfloat16).reshape(groups, 2 * slots, -1)
        msg = lax.all_to_all(msg, "corpus", split_axis=0, concat_axis=0, tiled=True)
        return msg.reshape(groups * 2 * slots, -1)

    block_granules = block_rows // GRAN
    sheet = jnp.swapaxes(sheet.reshape(groups, chips, 2, slots, SENT), 0, 1)
    valid = sheet[..., 0] >= 0
    lowest = sheet[..., 0] // GRAN + sheet[..., 1] // GRAN
    highest = sheet[..., 0] // GRAN + sheet[..., 2] // GRAN
    granules = jnp.arange(block_granules, dtype=jnp.int32)
    covers = valid[..., None] & (granules >= lowest[..., None]) & (granules <= highest[..., None])
    need = jnp.any(covers, axis=(1, 3))
    upto = jnp.sum((need[:, :, None, :] & (granules <= granules[:, None])).astype(jnp.int32), axis=-1)
    ranks = upto - need.astype(jnp.int32)
    hit = need[:, :, None, :] & (ranks[:, :, None, :] == granules[:, None])
    orders = jnp.sum(jnp.where(hit, granules, 0), axis=-1).reshape(chips, -1)
    marks = jnp.array([first // GRAN for first in firsts] + [block_granules], jnp.int32)
    bounds = jnp.sum((need[:, :, None, :] & (granules < marks[:, None])).astype(jnp.int32), axis=-1)
    bounds = bounds.reshape(chips, -1)
    before_low = need[:, None, :, None, :] & (granules < lowest[..., None])
    rank_low = jnp.sum(before_low.astype(jnp.int32), axis=-1)
    rank_high = rank_low + highest - lowest
    absent = 2 * block_granules
    tables = jnp.stack(
        [
            jnp.where(valid, rank_low, absent),
            jnp.where(valid, rank_high, -1),
            sheet[..., 1],
            sheet[..., 2],
            sheet[..., 3],
        ],
        axis=-1,
    ).reshape(chips, -1)
    plans = lax.optimization_barrier([(tables[s], orders[s], bounds[s]) for s in range(chips)])

    kept_gate = pltpu.with_memory_space_constraint(w_gate, pltpu.VMEM)
    kept_up = pltpu.with_memory_space_constraint(w_up, pltpu.VMEM)
    parts = []
    near_pieces = [(i, firsts[i], own[i], sibling[i]) for i in range(len(own))]
    near_msg = run_block(plans[0], near_pieces, in_hbm(w_gate), in_hbm(w_up), None, width, slots, True)
    done = [near_msg]
    for s in range(1, chips):
        msg = None
        for i, direct in enumerate(far[s - 1]):
            if s == 1 and i == len(own) // 2 - 1:
                near_msg, _ = lax.optimization_barrier((near_msg, done[-1]))
                parts.append(send_back(near_msg))
                direct, _ = lax.optimization_barrier((direct, parts[0]))
            direct, _ = lax.optimization_barrier((direct, done[-1]))
            relayed = lax.ppermute(direct, "neur", swap)
            relayed, _ = lax.optimization_barrier((in_hbm(relayed), done[-1]))
            piece = (i, firsts[i], direct, relayed)
            msg = run_block(plans[s], [piece], kept_gate, kept_up, msg, width, slots, False)
            done.append(msg)
        parts.append(send_back(msg))

    if chips == 1:
        parts.append(send_back(near_msg))
    where = (phase * groups + owner_group) * 2 * slots + rel * slots + rank
    return collect(where, shift, hit_mask, parts, local_width)


def solution(mesh):
    placed = (
        P(("corpus", "neur"), None),
        P(),
        P(None, "neur"),
        P(None, "neur"),
        P(("corpus", "neur")),
        P(("corpus", "neur")),
        P(("corpus", "neur"), None),
    )
    return jax.shard_map(
        per_device,
        mesh=mesh,
        in_specs=placed,
        out_specs=(P(("corpus", "neur"), None), P(("corpus", "neur"), None)),
        check_vma=False,
    )
```

time: 963 us -> 266 us (0.28)
  waiting for transfers between devices: 749 us -> 83.9 us
  Pallas kernels: 0 us -> 113 us
  matrix products: 68.8 us -> 0 us
  local copies, waits for them, and re-layouts: 73.5 us -> 27.6 us
  other arithmetic: 51.8 us -> 6.12 us
  starting transfers between devices: 4.63 us -> 32.6 us
  blocking collectives: 14.3 us -> 0 us
    all_to_all x1 -> x3, waiting for transfers between devices: 749 us -> 7.86 us  [the longest x2 7.85 us: send_back(): msg = lax.all_to_all(msg, 'corpus', split_axis=0, concat_axis=0, tiled=True)]
    pallas_call x0 -> x10, Pallas kernels: none -> 113 us  [the longest x7 96.1 us: run_block(): pl.pallas_call(functools.partial(block_kernel, spans=spans, slots_rel=slo...]
    ppermute x0 -> x18, waiting for transfers between devices: none -> 76.1 us  [the longest x6 56.8 us: per_device(): pieces.append(in_hbm(lax.ppermute(piece, 'neur', ring)))]
    gather x2 -> x0, local copies, waits for them, and re-layouts: 72.1 us -> none  [the longest x1 60.3 us: cut_windows(): taken = jnp.take(resid, row_ids.reshape(-1), axis=0)]
    dot_general x2 -> x0, matrix products: 68.8 us -> none  [the longest x1 37.3 us: normed_acts(): upward = jnp.dot(normed, w_up, preferred_element_type=jnp.float32)]
    unnamed x8 -> x50, local copies, waits for them, and re-layouts: 0.77 us -> 25.1 us
    select_n x3 -> x1, other arithmetic: 23.2 us -> 0.03 us  [per_device(): jnp.where(valid, rank_low, absent)]
    all_to_all x1 -> x3, starting transfers between devices: 4.63 us -> 19.2 us  [the longest x2 11.9 us: send_back(): msg = lax.all_to_all(msg, 'corpus', split_axis=0, concat_axis=0, tiled=True)]
  transfers between devices with their start and end apart: 1 -> 21, of which waited for: 1 -> 15; matrix products, arithmetic and copies ran while one was open for 0% -> 1% of each run, Pallas kernels for 0% -> 39%
where the time goes in v1:
time: 266 us; the launch traced here: 265 us
  Pallas kernels  113 us (42%)
  waiting for transfers between devices  83.9 us (32%)
  starting transfers between devices  32.6 us (12%)
  local copies, waits for them, and re-layouts  27.6 us (10%)
  other arithmetic  6.12 us (2%)
    pallas_call x7, Pallas kernels, run_block(): pl.pallas_call(functools.partial(block_kernel, spans=spans, slots_rel=slo...  96.1 us
    ppermute x6, waiting for transfers between devices, per_device(): pieces.append(in_hbm(lax.ppermute(piece, 'neur', ring)))  56.8 us
    unnamed x50, local copies, waits for them, and re-layouts  25.1 us
    pallas_call x2, Pallas kernels, norm_pieces(): pl.pallas_call(functools.partial(norm_kernel, starts=starts, counts=count...  15.1 us
    ppermute x6, waiting for transfers between devices, per_device(): relayed = lax.ppermute(direct, 'neur', swap)  12.8 us
    all_to_all x2, starting transfers between devices, send_back(): msg = lax.all_to_all(msg, 'corpus', split_axis=0, concat_axis=0, tiled=True)  11.9 us
    ppermute x6, starting transfers between devices, per_device(): pieces.append(in_hbm(lax.ppermute(piece, 'neur', ring)))  8.01 us
    all_to_all x2, waiting for transfers between devices, send_back(): msg = lax.all_to_all(msg, 'corpus', split_axis=0, concat_axis=0, tiled=True)  7.85 us
  transfers between devices with their start and end apart: 21, of which 15 were waited for; matrix products, arithmetic and copies ran while one was open for 1% of the time, Pallas kernels for 39%

profile of v1, /device:TPU:0, one launch (start us, length us, event | category | flops | bytes accessed | tf_op | source)
XLA Modules:
  0.0 264.5 jit_solution(2450665073143622327)
XLA Ops:
  4.6 7.3 %all-to-all-start = ((s32[8,1,64]{2,1,0:T(1,128)}), s32[8,1,64]{2,1,0:T(1,128)S(1)}, u32[]{:S(2)}, u32[]{:S(2)}) async-start(s32[8,1,64]{2,1,0:T(1,128)} %bitcast.4), calls=%async_computation | async-start | bytes 8192 | tf_op jit(solution)/shard_map/all_to_all | solution.py:327
  11.9 12.2 %norm_rows.3 = (bf16[256,4096]{1,0:T(8,128)(2,1)}, bf16[256,4096]{1,0:T(8,128)(2,1)}, bf16[192,4096]{1,0:T(8,128)(2,1)S(1)}, bf16[64,4096]{1,0:T(8,128)(2,1)}, bf16[64,4096]{1,0:T(8,128)(2,1)S(1)}) custom-call(bf16[1024,4096]{1,0:T(8,128)(2,1)} %rows.3, f32[4096]{0:T(1024)} %gain.3), custom_call_target="tpu_custom_call" | custom-call | tf_op jit(solution)/shard_map/norm_rows/pallas_call | solution.py:51
  30.7 3.9 %collective-permute-done.4.rest_10_ = bf16[64,4096]{1,0:T(8,128)(2,1)} collective-permute-done((bf16[64,4096]{1,0:T(8,128)(2,1)}, bf16[64,4096]{1,0:T(8,128)(2,1)}, u32[]{:S(2)}, u32[]{:S(2)}) %collective-permute-start.4) | collective-permute-done | bytes 524320 | tf_op jit(solution)/shard_map/ppermute | solution.py:307
  39.6 32.0 %block_acts.7 = f32[64,1664]{1,0:T(8,128)S(1)} custom-call(s32[320]{0:T(512)S(1)} %squeeze.23.table, s32[256]{0:T(256)S(1)} %get-tuple-element.28.order, s32[14]{0:T(128)S(1)} %squeeze.25.bounds, bf16[192,4096]{1,0:T(8,128)(2,1)} %copy-done.4, bf16[256,4096]{1,0:T(8,128)(2,1)} %get-tuple-element.30.rest_1_, bf16[256,4096]{1,0:T(8,128)(2,1)} %get-tuple-element.31.rest_2_, ...), custom_call_target="tpu_custom_call" | custom-call | flops 25769803776 | bytes 25165824 | tf_op jit(solution)/shard_map/block_acts/pallas_call | solution.py:210
  71.6 3.2 %collective-permute-done.7.rest_0_ = bf16[192,4096]{1,0:T(8,128)(2,1)S(1)} collective-permute-done((bf16[192,4096]{1,0:T(8,128)(2,1)S(1)}, bf16[192,4096]{1,0:T(8,128)(2,1)S(1)}, u32[]{:S(2)}, u32[]{:S(2)}) %collective-permute-start.7) | collective-permute-done | bytes 1572896 | tf_op jit(solution)/shard_map/ppermute | solution.py:305
  74.8 3.4 %collective-permute-done.8.rest_1_ = bf16[192,4096]{1,0:T(8,128)(2,1)S(1)} collective-permute-done((bf16[192,4096]{1,0:T(8,128)(2,1)S(1)}, bf16[192,4096]{1,0:T(8,128)(2,1)S(1)}, u32[]{:S(2)}, u32[]{:S(2)}) %collective-permute-start.8) | collective-permute-done | bytes 1572896 | tf_op jit(solution)/shard_map/ppermute | solution.py:381
  79.4 4.6 %copy-done = bf16[4096,1536]{1,0:T(8,128)(2,1)S(1)} copy-done((bf16[4096,1536]{1,0:T(8,128)(2,1)S(1)}, bf16[4096,1536]{1,0:T(8,128)(2,1)}, u32[]{:S(2)}) %copy-start) | copy-done | bytes 12582936
  83.9 4.6 %copy-done.2 = bf16[4096,1536]{1,0:T(8,128)(2,1)S(1)} copy-done((bf16[4096,1536]{1,0:T(8,128)(2,1)S(1)}, bf16[4096,1536]{1,0:T(8,128)(2,1)}, u32[]{:S(2)}) %copy-start.2) | copy-done | bytes 12582936
  88.5 13.6 %block_acts.8.rest_4_ = f32[64,1664]{1,0:T(8,128)S(1)} custom-call(s32[320]{0:T(512)S(1)} %squeeze.26.table, s32[256]{0:T(256)S(1)} %get-tuple-element.36.order, s32[14]{0:T(128)S(1)} %squeeze.28.bounds, bf16[192,4096]{1,0:T(8,128)(2,1)} %copy-done.14, bf16[192,4096]{1,0:T(8,128)(2,1)} %copy-done.15, bf16[4096,1536]{1,0:T(8,128)(2,1)S(1)} %copy-done, ...), custom_call_target="tpu_custom_call" | custom-call | flops 4831838208 | bytes 25165824 | tf_op jit(solution)/shard_map/block_acts/pallas_call | solution.py:210
  102.1 16.8 %collective-permute-done.6.rest_0_ = bf16[256,4096]{1,0:T(8,128)(2,1)S(1)} collective-permute-done((bf16[256,4096]{1,0:T(8,128)(2,1)}, bf16[256,4096]{1,0:T(8,128)(2,1)S(1)}, u32[]{:S(2)}, u32[]{:S(2)}) %collective-permute-start.6) | collective-permute-done | bytes 2097184 | tf_op jit(solution)/shard_map/ppermute | solution.py:305
  124.5 13.4 %block_acts.9.rest_4_ = f32[64,1664]{1,0:T(8,128)S(1)} custom-call(s32[320]{0:T(512)S(1)} %squeeze.26.table, s32[256]{0:T(256)S(1)} %get-tuple-element.36.order, s32[14]{0:T(128)S(1)} %squeeze.28.bounds, bf16[256,4096]{1,0:T(8,128)(2,1)} %copy-done.9, bf16[256,4096]{1,0:T(8,128)(2,1)} %copy-done.10, ...), custom_call_target="tpu_custom_call", output_to_operand_aliasing={{}: (7, {})} | custom-call | flops 6442450944 | bytes 25165824 | tf_op jit(solution)/shard_map/block_acts/pallas_call | solution.py:210
  138.6 6.1 %all-to-all-start.1 = ((bf16[8,8,1664]{2,1,0:T(8,128)(2,1)}), bf16[8,8,1664]{2,1,0:T(8,128)(2,1)S(1)}, u32[]{:S(2)}, u32[]{:S(2)}) async-start(bf16[8,8,1664]{2,1,0:T(8,128)(2,1)} %convert_bitcast_fusion.1), calls=%async_computation.1 | async-start | bytes 425984 | tf_op jit(solution)/shard_map/all_to_all | solution.py:333
  144.7 22.6 %collective-permute-done.13.rest_0_ = bf16[256,4096]{1,0:T(8,128)(2,1)} collective-permute-done((bf16[256,4096]{1,0:T(8,128)(2,1)}, bf16[256,4096]{1,0:T(8,128)(2,1)}, u32[]{:S(2)}, u32[]{:S(2)}) %collective-permute-start.13) | collective-permute-done | bytes 2097184 | tf_op jit(solution)/shard_map/ppermute | solution.py:305
  173.0 4.6 %copy-done.1 = bf16[4096,1536]{1,0:T(8,128)(2,1)S(1)} copy-done((bf16[4096,1536]{1,0:T(8,128)(2,1)S(1)}, bf16[4096,1536]{1,0:T(8,128)(2,1)}, u32[]{:S(2)}) %copy-start.1) | copy-done | bytes 12582936
  177.6 4.6 %copy-done.3 = bf16[4096,1536]{1,0:T(8,128)(2,1)S(1)} copy-done((bf16[4096,1536]{1,0:T(8,128)(2,1)S(1)}, bf16[4096,1536]{1,0:T(8,128)(2,1)}, u32[]{:S(2)}) %copy-start.3) | copy-done | bytes 12582936
  182.2 13.8 %block_acts.10.rest_4_ = f32[64,1664]{1,0:T(8,128)S(1)} custom-call(s32[320]{0:T(512)S(1)} %squeeze.26.table, s32[256]{0:T(256)S(1)} %get-tuple-element.36.order, s32[14]{0:T(128)S(1)} %squeeze.28.bounds, bf16[256,4096]{1,0:T(8,128)(2,1)} %collective-permute-done.13.rest_0_, bf16[256,4096]{1,0:T(8,128)(2,1)} %copy-done.11, ...), custom_call_target="tpu_custom_call", output_to_operand_aliasing={{}: (7, {})} | custom-call | flops 6442450944 | bytes 25165824 | tf_op jit(solution)/shard_map/block_acts/pallas_call | solution.py:210
  195.9 8.2 %collective-permute-done.12.rest_0_ = bf16[192,4096]{1,0:T(8,128)(2,1)S(1)} collective-permute-done((bf16[192,4096]{1,0:T(8,128)(2,1)S(1)}, bf16[192,4096]{1,0:T(8,128)(2,1)S(1)}, u32[]{:S(2)}, u32[]{:S(2)}) %collective-permute-start.12) | collective-permute-done | bytes 1572896 | tf_op jit(solution)/shard_map/ppermute | solution.py:305
  208.7 7.8 %block_acts.11.rest_4_ = f32[64,1664]{1,0:T(8,128)S(1)} custom-call(s32[320]{0:T(512)S(1)} %squeeze.26.table, s32[256]{0:T(256)S(1)} %get-tuple-element.36.order, s32[14]{0:T(128)S(1)} %squeeze.28.bounds, bf16[192,4096]{1,0:T(8,128)(2,1)} %copy-done.12, bf16[192,4096]{1,0:T(8,128)(2,1)} %copy-done.13, ...), custom_call_target="tpu_custom_call", output_to_operand_aliasing={{}: (7, {})} | custom-call | flops 4831838208 | bytes 25165824 | tf_op jit(solution)/shard_map/block_acts/pallas_call | solution.py:210
  218.7 4.1 %collective-permute-start.16 = (bf16[64,4096]{1,0:T(8,128)(2,1)S(1)}, bf16[64,4096]{1,0:T(8,128)(2,1)S(1)}, u32[]{:S(2)}, u32[]{:S(2)}) collective-permute-start(bf16[64,4096]{1,0:T(8,128)(2,1)S(1)} %collective-permute-done.11.rest_0_), channel_id=1, source_target_pairs={{0,1},{1,0},{2,3},{3,2},{4,5},{5,4},{6,7},{7,6},{8,9},{9,8},{10,11... | collective-permute-start | bytes 1572872 | tf_op jit(solution)/shard_map/ppermute | solution.py:381
  225.1 7.7 %block_acts.12.rest_4_ = f32[64,1664]{1,0:T(8,128)S(1)} custom-call(s32[320]{0:T(512)S(1)} %squeeze.26.table, s32[256]{0:T(256)S(1)} %get-tuple-element.36.order, s32[14]{0:T(128)S(1)} %squeeze.28.bounds, bf16[64,4096]{1,0:T(8,128)(2,1)} %copy-done.16, bf16[64,4096]{1,0:T(8,128)(2,1)} %copy-done.18, ...), custom_call_target="tpu_custom_call", output_to_operand_aliasing={{}: (7, {})} | custom-call | flops 1610612736 | bytes 25165824 | tf_op jit(solution)/shard_map/block_acts/pallas_call | solution.py:210
  232.9 3.8 %collective-permute-done.10.rest_0_ = bf16[64,4096]{1,0:T(8,128)(2,1)S(1)} collective-permute-done((bf16[64,4096]{1,0:T(8,128)(2,1)S(1)}, bf16[64,4096]{1,0:T(8,128)(2,1)S(1)}, u32[]{:S(2)}, u32[]{:S(2)}) %collective-permute-start.10) | collective-permute-done | bytes 524320 | tf_op jit(solution)/shard_map/ppermute | solution.py:305
  239.5 7.9 %block_acts.13 = f32[64,1664]{1,0:T(8,128)S(1)} custom-call(s32[320]{0:T(512)S(1)} %squeeze.26.table, s32[256]{0:T(256)S(1)} %get-tuple-element.36.order, s32[14]{0:T(128)S(1)} %squeeze.28.bounds, bf16[64,4096]{1,0:T(8,128)(2,1)} %copy-done.17, bf16[64,4096]{1,0:T(8,128)(2,1)} %copy-done.19, ...), custom_call_target="tpu_custom_call", output_to_operand_aliasing={{}: (7, {})} | custom-call | flops 1610612736 | bytes 25165824 | tf_op jit(solution)/shard_map/block_acts/pallas_call | solution.py:210
  248.1 5.8 %all-to-all-start.2 = ((bf16[8,8,1664]{2,1,0:T(8,128)(2,1)}), bf16[8,8,1664]{2,1,0:T(8,128)(2,1)S(1)}, u32[]{:S(2)}, u32[]{:S(2)}) async-start(bf16[8,8,1664]{2,1,0:T(8,128)(2,1)} %convert_bitcast_fusion), calls=%async_computation.2 | async-start | bytes 425984 | tf_op jit(solution)/shard_map/all_to_all | solution.py:333
  253.9 7.9 %all-to-all-done.2 = bf16[8,8,1664]{2,1,0:T(8,128)(2,1)S(1)} async-done(((bf16[8,8,1664]{2,1,0:T(8,128)(2,1)}), bf16[8,8,1664]{2,1,0:T(8,128)(2,1)S(1)}, u32[]{:S(2)}, u32[]{:S(2)}) %all-to-all-start.2) | async-done | bytes 213024 | tf_op jit(solution)/shard_map/all_to_all | solution.py:333
  (119 shorter events, 43.8 us)
Async XLA Ops:
  4.6 23.7 %all-to-all-start = ((s32[8,1,64]{2,1,0:T(1,128)}), s32[8,1,64]{2,1,0:T(1,128)S(1)}, u32[]{:S(2)}, u32[]{:S(2)}) async-start(s32[8,1,64]{2,1,0:T(1,128)} %bitcast.4), calls=%async_computation | async-start | bytes 8192 | tf_op jit(solution)/shard_map/all_to_all | solution.py:327
  24.2 15.4 %collective-permute-start.1 = (bf16[256,4096]{1,0:T(8,128)(2,1)}, bf16[256,4096]{1,0:T(8,128)(2,1)}, u32[]{:S(2)}, u32[]{:S(2)}) collective-permute-start(bf16[256,4096]{1,0:T(8,128)(2,1)} %get-tuple-element.30.rest_1_), channel_id=1, source_target_pairs={{0,1},{1,0},{2,3},{3,2},{4,5},{5,4},{6,7},{7,6},{8,9},{9,8},{10,11... | collective-permute-start | bytes 6291464 | tf_op jit(solution)/shard_map/ppermute | solution.py:307
  24.2 15.4 %collective-permute-start.2 = (bf16[256,4096]{1,0:T(8,128)(2,1)}, bf16[256,4096]{1,0:T(8,128)(2,1)}, u32[]{:S(2)}, u32[]{:S(2)}) collective-permute-start(bf16[256,4096]{1,0:T(8,128)(2,1)} %get-tuple-element.31.rest_2_), channel_id=1, source_target_pairs={{0,1},{1,0},{2,3},{3,2},{4,5},{5,4},{6,7},{7,6},{8,9},{9,8},{10,11... | collective-permute-start | bytes 6291464 | tf_op jit(solution)/shard_map/ppermute | solution.py:307
  24.7 14.4 %collective-permute-start.3 = (bf16[192,4096]{1,0:T(8,128)(2,1)S(1)}, bf16[192,4096]{1,0:T(8,128)(2,1)}, u32[]{:S(2)}, u32[]{:S(2)}) collective-permute-start(bf16[192,4096]{1,0:T(8,128)(2,1)S(1)} %get-tuple-element.32.rest_3_), channel_id=1, source_target_pairs={{0,1},{1,0},{2,3},{3,2},{4,5},{5,4},{6,7},{7,6},{8,9},{9,8},{10,11... | collective-permute-start | bytes 4718600 | tf_op jit(solution)/shard_map/ppermute | solution.py:307
  24.8 9.9 %collective-permute-start.4 = (bf16[64,4096]{1,0:T(8,128)(2,1)}, bf16[64,4096]{1,0:T(8,128)(2,1)}, u32[]{:S(2)}, u32[]{:S(2)}) collective-permute-start(bf16[64,4096]{1,0:T(8,128)(2,1)} %get-tuple-element.33.rest_4_), channel_id=1, source_target_pairs={{0,1},{1,0},{2,3},{3,2},{4,5},{5,4},{6,7},{7,6},{8,9},{9,8},{10,11... | collective-permute-start | bytes 1572872 | tf_op jit(solution)/shard_map/ppermute | solution.py:307
  28.1 11.5 %collective-permute-start = (bf16[192,4096]{1,0:T(8,128)(2,1)S(1)}, bf16[192,4096]{1,0:T(8,128)(2,1)}, u32[]{:S(2)}, u32[]{:S(2)}) collective-permute-start(bf16[192,4096]{1,0:T(8,128)(2,1)S(1)} %norm_rows.2.rest_0_), channel_id=1, source_target_pairs={{0,1},{1,0},{2,3},{3,2},{4,5},{5,4},{6,7},{7,6},{8,9},{9,8},{10,11... | collective-permute-start | bytes 4718600 | tf_op jit(solution)/shard_map/ppermute | solution.py:307
  34.7 2.9 %collective-permute-start.5 = (bf16[64,4096]{1,0:T(8,128)(2,1)}, bf16[64,4096]{1,0:T(8,128)(2,1)S(1)}, u32[]{:S(2)}, u32[]{:S(2)}) collective-permute-start(bf16[64,4096]{1,0:T(8,128)(2,1)} %copy-done.7), channel_id=1, source_target_pairs={{0,1},{1,0},{2,3},{3,2},{4,5},{5,4},{6,7},{7,6},{8,9},{9,8},{10,11... | collective-permute-start | bytes 1572872 | tf_op jit(solution)/shard_map/ppermute | solution.py:307
  37.5 37.3 %collective-permute-start.7 = (bf16[192,4096]{1,0:T(8,128)(2,1)S(1)}, bf16[192,4096]{1,0:T(8,128)(2,1)S(1)}, u32[]{:S(2)}, u32[]{:S(2)}) collective-permute-start(bf16[192,4096]{1,0:T(8,128)(2,1)S(1)} %norm_rows.2.rest_0_), channel_id=1, source_target_pairs={{0,2},{1,3},{2,0},{3,1},{4,6},{5,7},{6,4},{7,5},{8,10},{9,11},{10,... | collective-permute-start | bytes 4718600 | tf_op jit(solution)/shard_map/ppermute | solution.py:305
  39.0 79.9 %collective-permute-start.6 = (bf16[256,4096]{1,0:T(8,128)(2,1)}, bf16[256,4096]{1,0:T(8,128)(2,1)S(1)}, u32[]{:S(2)}, u32[]{:S(2)}) collective-permute-start(bf16[256,4096]{1,0:T(8,128)(2,1)} %get-tuple-element.30.rest_1_), channel_id=1, source_target_pairs={{0,2},{1,3},{2,0},{3,1},{4,6},{5,7},{6,4},{7,5},{8,10},{9,11},{10,... | collective-permute-start | bytes 6291464 | tf_op jit(solution)/shard_map/ppermute | solution.py:305
  74.8 3.4 %collective-permute-start.8 = (bf16[192,4096]{1,0:T(8,128)(2,1)S(1)}, bf16[192,4096]{1,0:T(8,128)(2,1)S(1)}, u32[]{:S(2)}, u32[]{:S(2)}) collective-permute-start(bf16[192,4096]{1,0:T(8,128)(2,1)S(1)} %collective-permute-done.7.rest_0_), channel_id=1, source_target_pairs={{0,1},{1,0},{2,3},{3,2},{4,5},{5,4},{6,7},{7,6},{8,9},{9,8},{10,11... | collective-permute-start | bytes 4718600 | tf_op jit(solution)/shard_map/ppermute | solution.py:381
  102.1 65.2 %copy-start.6 = (bf16[192,4096]{1,0:T(8,128)(2,1)S(1)}, bf16[192,4096]{1,0:T(8,128)(2,1)}, u32[]{:S(2)}) copy-start(bf16[192,4096]{1,0:T(8,128)(2,1)} %copy-done.5) | copy-start | bytes 4718596
  118.9 4.2 %collective-permute-start.9 = (bf16[256,4096]{1,0:T(8,128)(2,1)S(1)}, bf16[256,4096]{1,0:T(8,128)(2,1)S(1)}, u32[]{:S(2)}, u32[]{:S(2)}) collective-permute-start(bf16[256,4096]{1,0:T(8,128)(2,1)S(1)} %collective-permute-done.6.rest_0_), channel_id=1, source_target_pairs={{0,1},{1,0},{2,3},{3,2},{4,5},{5,4},{6,7},{7,6},{8,9},{9,8},{10,11... | collective-permute-start | bytes 6291464 | tf_op jit(solution)/shard_map/ppermute | solution.py:381
  118.9 48.4 %collective-permute-start.13 = (bf16[256,4096]{1,0:T(8,128)(2,1)}, bf16[256,4096]{1,0:T(8,128)(2,1)}, u32[]{:S(2)}, u32[]{:S(2)}) collective-permute-start(bf16[256,4096]{1,0:T(8,128)(2,1)} %get-tuple-element.31.rest_2_), channel_id=1, source_target_pairs={{0,2},{1,3},{2,0},{3,1},{4,6},{5,7},{6,4},{7,5},{8,10},{9,11},{10,... | collective-permute-start | bytes 6291464 | tf_op jit(solution)/shard_map/ppermute | solution.py:305
  138.6 28.7 %all-to-all-start.1 = ((bf16[8,8,1664]{2,1,0:T(8,128)(2,1)}), bf16[8,8,1664]{2,1,0:T(8,128)(2,1)S(1)}, u32[]{:S(2)}, u32[]{:S(2)}) async-start(bf16[8,8,1664]{2,1,0:T(8,128)(2,1)} %convert_bitcast_fusion.1), calls=%async_computation.1 | async-start | bytes 425984 | tf_op jit(solution)/shard_map/all_to_all | solution.py:333
  167.3 4.4 %collective-permute-start.14 = (bf16[256,4096]{1,0:T(8,128)(2,1)}, bf16[256,4096]{1,0:T(8,128)(2,1)S(1)}, u32[]{:S(2)}, u32[]{:S(2)}) collective-permute-start(bf16[256,4096]{1,0:T(8,128)(2,1)} %collective-permute-done.13.rest_0_), channel_id=1, source_target_pairs={{0,1},{1,0},{2,3},{3,2},{4,5},{5,4},{6,7},{7,6},{8,9},{9,8},{10,11... | collective-permute-start | bytes 6291464 | tf_op jit(solution)/shard_map/ppermute | solution.py:381
  167.3 36.8 %collective-permute-start.12 = (bf16[192,4096]{1,0:T(8,128)(2,1)S(1)}, bf16[192,4096]{1,0:T(8,128)(2,1)S(1)}, u32[]{:S(2)}, u32[]{:S(2)}) collective-permute-start(bf16[192,4096]{1,0:T(8,128)(2,1)S(1)} %copy-done.6), channel_id=1, source_target_pairs={{0,2},{1,3},{2,0},{3,1},{4,6},{5,7},{6,4},{7,5},{8,10},{9,11},{10,... | collective-permute-start | bytes 4718600 | tf_op jit(solution)/shard_map/ppermute | solution.py:305
  195.9 26.8 %copy-start.8 = (bf16[64,4096]{1,0:T(8,128)(2,1)S(1)}, bf16[64,4096]{1,0:T(8,128)(2,1)}, u32[]{:S(2)}) copy-start(bf16[64,4096]{1,0:T(8,128)(2,1)} %copy-done.7) | copy-start | bytes 1572868
  204.1 3.4 %collective-permute-start.15 = (bf16[192,4096]{1,0:T(8,128)(2,1)S(1)}, bf16[192,4096]{1,0:T(8,128)(2,1)S(1)}, u32[]{:S(2)}, u32[]{:S(2)}) collective-permute-start(bf16[192,4096]{1,0:T(8,128)(2,1)S(1)} %collective-permute-done.12.rest_0_), channel_id=1, source_target_pairs={{0,1},{1,0},{2,3},{3,2},{4,5},{5,4},{6,7},{7,6},{8,9},{9,8},{10,11... | collective-permute-start | bytes 4718600 | tf_op jit(solution)/shard_map/ppermute | solution.py:381
  204.1 14.5 %collective-permute-start.11 = (bf16[64,4096]{1,0:T(8,128)(2,1)}, bf16[64,4096]{1,0:T(8,128)(2,1)S(1)}, u32[]{:S(2)}, u32[]{:S(2)}) collective-permute-start(bf16[64,4096]{1,0:T(8,128)(2,1)} %get-tuple-element.33.rest_4_), channel_id=1, source_target_pairs={{0,2},{1,3},{2,0},{3,1},{4,6},{5,7},{6,4},{7,5},{8,10},{9,11},{10,... | collective-permute-start | bytes 1572872 | tf_op jit(solution)/shard_map/ppermute | solution.py:305
  218.7 5.6 %collective-permute-start.16 = (bf16[64,4096]{1,0:T(8,128)(2,1)S(1)}, bf16[64,4096]{1,0:T(8,128)(2,1)S(1)}, u32[]{:S(2)}, u32[]{:S(2)}) collective-permute-start(bf16[64,4096]{1,0:T(8,128)(2,1)S(1)} %collective-permute-done.11.rest_0_), channel_id=1, source_target_pairs={{0,1},{1,0},{2,3},{3,2},{4,5},{5,4},{6,7},{7,6},{8,9},{9,8},{10,11... | collective-permute-start | bytes 1572872 | tf_op jit(solution)/shard_map/ppermute | solution.py:381
  222.8 14.0 %collective-permute-start.10 = (bf16[64,4096]{1,0:T(8,128)(2,1)S(1)}, bf16[64,4096]{1,0:T(8,128)(2,1)S(1)}, u32[]{:S(2)}, u32[]{:S(2)}) collective-permute-start(bf16[64,4096]{1,0:T(8,128)(2,1)S(1)} %copy-done.8), channel_id=1, source_target_pairs={{0,2},{1,3},{2,0},{3,1},{4,6},{5,7},{6,4},{7,5},{8,10},{9,11},{10,... | collective-permute-start | bytes 1572872 | tf_op jit(solution)/shard_map/ppermute | solution.py:305
  232.9 20.9 %copy-start.20 = (s32[64,32]{0,1:T(8,128)S(1)}, s32[64,32]{0,1:T(8,128)}, u32[]{:S(2)}) copy-start(s32[64,32]{0,1:T(8,128)} %param.15) | copy-start | bytes 24580
  236.7 1.9 collective-permute-start.17
  248.1 13.7 %all-to-all-start.2 = ((bf16[8,8,1664]{2,1,0:T(8,128)(2,1)}), bf16[8,8,1664]{2,1,0:T(8,128)(2,1)S(1)}, u32[]{:S(2)}, u32[]{:S(2)}) async-start(bf16[8,8,1664]{2,1,0:T(8,128)(2,1)} %convert_bitcast_fusion), calls=%async_computation.2 | async-start | bytes 425984 | tf_op jit(solution)/shard_map/all_to_all | solution.py:333
  (21 other events, 72.0 us)

commit v2 on v1

--- a/solution.py
+++ b/solution.py
@@ -12,8 +12,11 @@
 GRAN = 8
 LANES = 128
 SENT = 4
-FIELDS = 5
-PIECES = (3, 4, 4, 3, 1, 1)
+FIELDS = 6
+UNITS = 16
+FLIP = 1 << 20
+DENSE = 2
+PACKED = (3, 3, 2, 1, 1)
 STRIP = 128
 ROOM = 13 * 1024 * 1024
 ROOM_STREAMED = 46 * 1024 * 1024
@@ -64,8 +67,57 @@
     )(resid, gain)
 
 
-def block_kernel(table, order, bounds, *rest, spans, slots_rel, fresh, streamed):
-    rows, rest = rest[:2 * len(spans)], rest[2 * len(spans):]
+def pack_kernel(listing, own, sibling, *rest, starts, block_granules):
+    outs, sem = rest[:-1], rest[-1]
+
+    def granule_copy(source, at, out, to):
+        return pltpu.make_async_copy(
+            source.at[pl.ds(pl.multiple_of(at * GRAN, GRAN), GRAN), :],
+            out.at[pl.ds(pl.multiple_of(to * GRAN, GRAN), GRAN), :],
+            sem,
+        )
+
+    for out, start in zip(outs, starts):
+
+        def one(j, carry):
+            at = listing[start + j]
+
+            @pl.when(at < block_granules)
+            def _():
+                granule_copy(own, at, out, j).start()
+
+            @pl.when(at >= block_granules)
+            def _():
+                granule_copy(sibling, at - block_granules, out, j).start()
+
+            return carry
+
+        lax.fori_loop(0, out.shape[0] // GRAN, one, 0)
+    for out in outs:
+
+        def settle(j, carry):
+            granule_copy(own, 0, out, 0).wait()
+            return carry
+
+        lax.fori_loop(0, out.shape[0] // GRAN, settle, 0)
+
+
+def pack_rows(listing, own, sibling, starts, sizes, block_granules):
+    hbm = pl.BlockSpec(memory_space=pltpu.HBM)
+    return pl.pallas_call(
+        functools.partial(pack_kernel, starts=starts, block_granules=block_granules),
+        in_specs=[pl.BlockSpec(memory_space=pltpu.SMEM), hbm, hbm],
+        out_specs=[pl.BlockSpec(memory_space=pltpu.VMEM)] * len(sizes),
+        out_shape=[jax.ShapeDtypeStruct((size * GRAN, own.shape[1]), own.dtype) for size in sizes],
+        scratch_shapes=[pltpu.SemaphoreType.DMA],
+        compiler_params=pltpu.CompilerParams(vmem_limit_bytes=20 * 1024 * 1024),
+        name="pack_rows",
+    )(listing, own, sibling)
+
+
+def block_kernel(table, order, bounds, *rest, runs, fresh, streamed):
+    row_refs = sum(len(run[2]) for run in runs)
+    rows, rest = rest[:row_refs], rest[row_refs:]
     w_gate, w_up, *rest = rest
     if fresh:
         before = None
@@ -76,13 +128,9 @@
     tile = w_gate.shape[1] if streamed else tile_of(local_width)
     slot_count = msg.shape[0]
     reach = acts.shape[0] - stack.shape[0]
-    marks = bounds.shape[0] // 2
-    listed = order.shape[0] // 2
-    first_mark, last_mark = spans[0][0], spans[-1][0] + 1
-    bases = [bounds[half * marks + first_mark] for half in range(2)]
-    ends = [bounds[half * marks + last_mark] for half in range(2)]
-    shifts = [0 - bases[0], ends[0] - bases[0] - bases[1]]
-    total = ends[1] + shifts[1]
+    base = bounds[runs[0][0]]
+    end = bounds[runs[-1][0] + 1]
+    total = end - base
 
     def granule_copy(i, at, to):
         return pltpu.make_async_copy(
@@ -92,15 +140,25 @@
         )
 
     def load_rows():
-        for half in range(2):
-            for i, (mark, first) in enumerate(spans):
-
-                def one(rank, carry):
-                    at = order[half * listed + rank] - first
-                    granule_copy(half * len(spans) + i, at, rank + shifts[half]).start()
-                    return carry
-
-                lax.fori_loop(bounds[half * marks + mark], bounds[half * marks + mark + 1], one, 0)
+        for mark, first, which in runs:
+
+            def one(rank, carry):
+                at = order[rank]
+                if len(which) == 1:
+                    granule_copy(which[0], at - first, rank - base).start()
+                else:
+
+                    @pl.when(at < FLIP)
+                    def _():
+                        granule_copy(which[0], at - first, rank - base).start()
+
+                    @pl.when(at >= FLIP)
+                    def _():
+                        granule_copy(which[1], at - FLIP - first, rank - base).start()
+
+                return carry
+
+            lax.fori_loop(bounds[mark], bounds[mark + 1], one, 0)
         if fresh:
             msg[...] = jnp.full(msg.shape, -jnp.inf, jnp.float32)
         else:
@@ -132,19 +190,16 @@
         def one_slot(slot, carry):
             rank_low = table[slot * FIELDS]
             rank_high = table[slot * FIELDS + 1]
-            second = (slot // slots_rel) % 2 == 1
-            base = jnp.where(second, bases[1], bases[0])
-            end = jnp.where(second, ends[1], ends[0])
 
             @pl.when((rank_high >= base) & (rank_low < end))
             def _():
-                low = table[slot * FIELDS + 2]
-                high = table[slot * FIELDS + 3]
-                neuron = table[slot * FIELDS + 4]
+                low = table[slot * FIELDS + 3]
+                high = table[slot * FIELDS + 4]
+                neuron = table[slot * FIELDS + 5]
                 rank = jnp.maximum(rank_low, base)
                 here = (jnp.minimum(rank_high + 1, end) - rank) * GRAN
-                past = (rank - rank_low) * GRAN + low // GRAN * GRAN
-                top = pl.multiple_of((rank + jnp.where(second, shifts[1], shifts[0])) * GRAN, GRAN)
+                past = (rank - rank_low) * GRAN + table[slot * FIELDS + 2]
+                top = pl.multiple_of((rank - base) * GRAN, GRAN)
                 live = (local >= low - past) & (local <= high - past) & (local < here)
                 best = jnp.max(jnp.where(live, acts[pl.ds(top, reach), :], -jnp.inf), axis=0, keepdims=True)
                 column = pl.multiple_of(neuron // LANES * LANES, LANES)
@@ -180,12 +235,15 @@
     return 256 if local_width % 256 == 0 else local_width
 
 
-def run_block(plan, pieces, w_gate, w_up, before, width, slots_rel, streamed):
+def run_block(plan, pieces, w_gate, w_up, before, width, streamed):
     table, order, bounds = plan
     model_width, local_width = w_gate.shape
     slot_count = table.shape[0] // FIELDS
-    spans = [(mark, first // GRAN) for mark, first, _, _ in pieces]
-    rows = [p[2] for p in pieces] + [p[3] for p in pieces]
+    rows = []
+    runs = []
+    for mark, first, sources in pieces:
+        runs.append((mark, first, [len(rows) + i for i in range(len(sources))]))
+        rows.extend(sources)
     row_count = sum(r.shape[0] for r in rows)
     reach = (width + 2 * GRAN - 2) // GRAN * GRAN
     fresh = before is None
@@ -210,8 +268,7 @@
     return pl.pallas_call(
         functools.partial(
             block_kernel,
-            spans=spans,
-            slots_rel=slots_rel,
+            runs=runs,
             fresh=fresh,
             streamed=streamed,
         ),
@@ -272,6 +329,19 @@
     )(where, shift, mask, *parts)
 
 
+def make_plan(flags, codes, cuts, starts, lengths, pasts, extra):
+    places = jnp.arange(flags.shape[0], dtype=jnp.int32)
+    ranks = jnp.sum((flags & (places < places[:, None])).astype(jnp.int32), axis=1)
+    order = jnp.sum(jnp.where(flags & (ranks == places[:, None]), codes, 0), axis=1)
+    bounds = jnp.sum((flags & cuts).astype(jnp.int32), axis=1)
+    first = jnp.sum((flags & (places < starts[:, None])).astype(jnp.int32), axis=1)
+    some = lengths > 0
+    table = jnp.stack(
+        [jnp.where(some, first, 2 * FLIP), jnp.where(some, first + lengths - 1, -1), pasts, *extra], axis=1
+    )
+    return table.reshape(-1), order, bounds
+
+
 def in_hbm(x):
     return pltpu.with_memory_space_constraint(x, pltpu.HBM)
 
@@ -290,21 +360,21 @@
     chips = columns // 2
     gain = in_hbm(norm_gain)
 
-    unit = block_rows // 16
-    sizes = [unit * n for n in PIECES]
-    firsts = [sum(sizes[:i]) for i in range(len(sizes))]
-    own = norm_pieces(resid, gain, 0, sizes[:1], unit)
-    own = own + norm_pieces(resid, gain, sizes[0], sizes[1:], unit)
-    own = [in_hbm(piece) for piece in own]
+    unit = block_rows // UNITS
+    dense_rows = DENSE * unit
+    own_first = norm_pieces(resid, gain, 0, [dense_rows], unit)[0]
+    own_rest = norm_pieces(resid, gain, dense_rows, [block_rows - dense_rows], dense_rows)[0]
+    own_first, own_rest = in_hbm(own_first), in_hbm(own_rest)
     swap = [(i, i ^ 1) for i in range(columns)]
-    far = []
+
+    def forward(s):
+        return [(i, (i + 2 * s) % columns) for i in range(columns)]
+
+    far_first = []
     for s in range(1, chips):
-        ring = [(i, (i + 2 * s) % columns) for i in range(columns)]
-        pieces = []
-        for piece in own:
-            pieces.append(in_hbm(lax.ppermute(piece, "neur", ring)))
-        far.append(pieces)
-    sibling = [in_hbm(lax.ppermute(piece, "neur", swap)) for piece in own]
+        far_first.append(in_hbm(lax.ppermute(own_first, "neur", forward(s))))
+    sibling_first = in_hbm(lax.ppermute(own_first, "neur", swap))
+    sibling_rest = in_hbm(lax.ppermute(own_rest, "neur", swap))
 
     owner = hit_start // block_rows
     owner_group = owner // columns
@@ -334,6 +404,9 @@
         return msg.reshape(groups * 2 * slots, -1)
 
     block_granules = block_rows // GRAN
+    both = 2 * block_granules
+    dense = dense_rows // GRAN
+    core = member % 2
     sheet = jnp.swapaxes(sheet.reshape(groups, chips, 2, slots, SENT), 0, 1)
     valid = sheet[..., 0] >= 0
     lowest = sheet[..., 0] // GRAN + sheet[..., 1] // GRAN
@@ -341,47 +414,126 @@
     granules = jnp.arange(block_granules, dtype=jnp.int32)
     covers = valid[..., None] & (granules >= lowest[..., None]) & (granules <= highest[..., None])
     need = jnp.any(covers, axis=(1, 3))
-    upto = jnp.sum((need[:, :, None, :] & (granules <= granules[:, None])).astype(jnp.int32), axis=-1)
-    ranks = upto - need.astype(jnp.int32)
-    hit = need[:, :, None, :] & (ranks[:, :, None, :] == granules[:, None])
-    orders = jnp.sum(jnp.where(hit, granules, 0), axis=-1).reshape(chips, -1)
-    marks = jnp.array([first // GRAN for first in firsts] + [block_granules], jnp.int32)
-    bounds = jnp.sum((need[:, :, None, :] & (granules < marks[:, None])).astype(jnp.int32), axis=-1)
-    bounds = bounds.reshape(chips, -1)
-    before_low = need[:, None, :, None, :] & (granules < lowest[..., None])
-    rank_low = jnp.sum(before_low.astype(jnp.int32), axis=-1)
-    rank_high = rank_low + highest - lowest
-    absent = 2 * block_granules
-    tables = jnp.stack(
-        [
-            jnp.where(valid, rank_low, absent),
-            jnp.where(valid, rank_high, -1),
-            sheet[..., 1],
-            sheet[..., 2],
-            sheet[..., 3],
-        ],
-        axis=-1,
-    ).reshape(chips, -1)
-    plans = lax.optimization_barrier([(tables[s], orders[s], bounds[s]) for s in range(chips)])
+    sides = jnp.broadcast_to(jnp.arange(2, dtype=jnp.int32)[:, None], (2, slots))
+    sides = jnp.broadcast_to(sides, (groups, 2, slots)).reshape(-1)
+    flat_valid = valid.reshape(chips, -1)
+    flat_low = lowest.reshape(chips, -1)
+    flat_high = highest.reshape(chips, -1)
+    fields = sheet.reshape(chips, -1, SENT)
+    extras = [[fields[s, :, 1], fields[s, :, 2], fields[s, :, 3]] for s in range(chips)]
+    places = jnp.arange(both, dtype=jnp.int32)
+    inside = places % block_granules
+
+    by_core = jnp.where(core == 0, need, need[:, ::-1]).astype(jnp.int32)
+    asked = by_core | lax.ppermute(by_core, "neur", swap)
+    received = [
+        lax.ppermute(asked[s], "neur", [(i, (i - 2 * s) % columns) for i in range(columns)]) for s in range(1, chips)
+    ]
+    sizes = [n * unit // GRAN for n in PACKED]
+    starts = [sum(sizes[:i]) for i in range(len(sizes))]
+    capacity = sum(sizes)
+    spare = block_granules - dense - capacity
+    listings = []
+    most = jnp.int32(0)
+    turn = jnp.arange(block_granules - dense, dtype=jnp.int32)
+    for s in range(1, chips):
+        flags = (received[s - 1].reshape(-1) > 0) & (inside >= dense)
+        ranks = jnp.sum((flags & (places < places[:, None])).astype(jnp.int32), axis=1)
+        most = jnp.maximum(most, jnp.sum(flags.astype(jnp.int32)))
+        most = jnp.maximum(most, jnp.sum(((asked[s].reshape(-1) > 0) & (inside >= dense)).astype(jnp.int32)))
+        source = inside - dense + jnp.where(places // block_granules == core, 0, block_granules)
+        picks = flags & (ranks == (2 * turn + core)[:, None])
+        listings.append(jnp.sum(jnp.where(picks, source, 0), axis=1))
+    counts = jnp.broadcast_to(most, (groups, LANES))
+    most = jnp.max(lax.all_to_all(counts, "corpus", split_axis=0, concat_axis=0, tiled=True))
+    if chips > 2:
+        most = lax.pmax(most, "neur")
+    over = most > 2 * capacity
+
+    cuts = jnp.stack([places < m for m in (0, dense, block_granules, block_granules + dense, both)])
+    near_plan = make_plan(
+        need[0].reshape(-1),
+        inside,
+        cuts,
+        sides * block_granules + flat_low[0],
+        jnp.where(flat_valid[0], flat_high[0] - flat_low[0] + 1, 0),
+        fields[0, :, 1] // GRAN * GRAN,
+        extras[0],
+    )
+    far_plans = []
+    for s in range(1, chips):
+        first_flags = need[s, :, :dense].reshape(-1)
+        first_places = jnp.arange(2 * dense, dtype=jnp.int32)
+        first_plan = make_plan(
+            first_flags,
+            first_places % dense,
+            jnp.stack([first_places < m for m in (0, dense, 2 * dense)]),
+            sides * dense + flat_low[s],
+            jnp.where(flat_valid[s], jnp.minimum(flat_high[s], dense - 1) - flat_low[s] + 1, 0),
+            fields[s, :, 1] // GRAN * GRAN,
+            extras[s],
+        )
+        flags = (asked[s].reshape(-1) > 0) & (inside >= dense)
+        ranks = jnp.sum((flags & (places < places[:, None])).astype(jnp.int32), axis=1)
+        codes = ranks // 2 + jnp.where(ranks % 2 == core, 0, FLIP)
+        begin = jnp.maximum(flat_low[s], dense)
+        packed_plan = make_plan(
+            (by_core[s].reshape(-1) > 0) & (inside >= dense),
+            codes,
+            jnp.stack([ranks // 2 < m for m in (*starts, capacity, both)]),
+            (sides ^ core) * block_granules + begin,
+            jnp.where(flat_valid[s], flat_high[s] - begin + 1, 0),
+            (fields[s, :, 1] // GRAN + begin - flat_low[s]) * GRAN,
+            extras[s],
+        )
+        far_plans.append((first_plan, packed_plan))
+    near_plan, far_plans, listings = lax.optimization_barrier((near_plan, far_plans, listings))
+
+    packed = []
+    for s in range(1, chips):
+        pieces = pack_rows(listings[s - 1], own_rest, sibling_rest, starts, sizes, block_granules)
+        sent = []
+        for piece in pieces:
+            sent.append(in_hbm(lax.ppermute(in_hbm(piece), "neur", forward(s))))
+        packed.append(sent)
 
     kept_gate = pltpu.with_memory_space_constraint(w_gate, pltpu.VMEM)
     kept_up = pltpu.with_memory_space_constraint(w_up, pltpu.VMEM)
+    far_gate, far_up = in_hbm(w_gate), in_hbm(w_up)
     parts = []
-    near_pieces = [(i, firsts[i], own[i], sibling[i]) for i in range(len(own))]
-    near_msg = run_block(plans[0], near_pieces, in_hbm(w_gate), in_hbm(w_up), None, width, slots, True)
+    near_pieces = [
+        (0, 0, [own_first]),
+        (1, dense, [own_rest]),
+        (2, 0, [sibling_first]),
+        (3, dense, [sibling_rest]),
+    ]
+    near_msg = run_block(near_plan, near_pieces, far_gate, far_up, None, width, True)
     done = [near_msg]
     for s in range(1, chips):
-        msg = None
-        for i, direct in enumerate(far[s - 1]):
-            if s == 1 and i == len(own) // 2 - 1:
-                near_msg, _ = lax.optimization_barrier((near_msg, done[-1]))
-                parts.append(send_back(near_msg))
-                direct, _ = lax.optimization_barrier((direct, parts[0]))
-            direct, _ = lax.optimization_barrier((direct, done[-1]))
+        first_plan, packed_plan = far_plans[s - 1]
+        direct, _ = lax.optimization_barrier((far_first[s - 1], done[-1]))
+        relayed = lax.ppermute(direct, "neur", swap)
+        if s == 1:
+            parts.append(send_back(near_msg))
+            relayed, _ = lax.optimization_barrier((relayed, parts[0]))
+        pieces = [(0, 0, [direct]), (1, 0, [in_hbm(relayed)])]
+        msg = run_block(first_plan, pieces, far_gate, far_up, None, width, True)
+
+        def leftover(msg):
+            piece = pack_rows(listings[s - 1], own_rest, sibling_rest, [capacity], [spare], block_granules)[0]
+            direct = in_hbm(lax.ppermute(piece, "neur", forward(s)))
+            relayed = in_hbm(lax.ppermute(direct, "neur", swap))
+            pieces = [(len(sizes), capacity, [direct, relayed])]
+            return run_block(packed_plan, pieces, far_gate, far_up, msg, width, True)
+
+        msg = lax.cond(over, leftover, lambda m: m, msg)
+        done.append(msg)
+        for i, direct in enumerate(packed[s - 1]):
+            direct, _ = lax.optimization_barrier((direct, done[-2]))
             relayed = lax.ppermute(direct, "neur", swap)
             relayed, _ = lax.optimization_barrier((in_hbm(relayed), done[-1]))
-            piece = (i, firsts[i], direct, relayed)
-            msg = run_block(plans[s], [piece], kept_gate, kept_up, msg, width, slots, False)
+            pieces = [(i, starts[i], [direct, relayed])]
+            msg = run_block(packed_plan, pieces, kept_gate, kept_up, msg, width, False)
             done.append(msg)
         parts.append(send_back(msg))
 

time: 266 us -> 232 us (0.87)
  the two profiles are of different devices: /device:TPU:0 before, /device:TPU:2 now
where the time goes in v2:
time: 232 us; the launch traced here: 231 us
  Pallas kernels  129 us (56%)
  starting transfers between devices  40.9 us (18%)
  waiting for transfers between devices  29 us (12%)
  local copies, waits for them, and re-layouts  20.8 us (9%)
  other arithmetic  7.4 us (3%)
  between operations  3.32 us (1%)
    pallas_call x7, Pallas kernels, run_block(): pl.pallas_call(functools.partial(block_kernel, runs=runs, fresh=fresh, st...  110 us
    all_to_all x2, starting transfers between devices, send_back(): msg = lax.all_to_all(msg, 'corpus', split_axis=0, concat_axis=0, tiled=True)  20.7 us
    unnamed x38, local copies, waits for them, and re-layouts  16 us
    all_to_all x2, waiting for transfers between devices, send_back(): msg = lax.all_to_all(msg, 'corpus', split_axis=0, concat_axis=0, tiled=True)  15.3 us
    pallas_call x2, Pallas kernels, norm_pieces(): pl.pallas_call(functools.partial(norm_kernel, starts=starts, counts=count...  11.8 us
    ppermute x1, waiting for transfers between devices, per_device(): asked = by_core | lax.ppermute(by_core, 'neur', swap)  7.77 us
    all_to_all x1, starting transfers between devices, per_device(): lax.all_to_all(counts, 'corpus', split_axis=0, concat_axis=0, tiled=True)  6.47 us
    all_to_all x1, starting transfers between devices, per_device(): lax.all_to_all(sheet.reshape(groups, -1), 'corpus', split_axis=0, concat_...  6.25 us
  transfers between devices with their start and end apart: 20, of which 5 were waited for; matrix products, arithmetic and copies ran while one was open for 4% of the time, Pallas kernels for 53%

profile of v2, /device:TPU:2, one launch (start us, length us, event | category | flops | bytes accessed | tf_op | source)
XLA Modules:
  0.0 230.7 jit_solution(16882527475220739812)
XLA Ops:
  0.7 1.8 norm_rows.2.rest_0_
  4.0 6.3 %all-to-all-start = ((s32[8,1,64]{2,1,0:T(1,128)}), s32[8,1,64]{2,1,0:T(1,128)S(1)}, u32[]{:S(2)}, u32[]{:S(2)}) async-start(s32[8,1,64]{2,1,0:T(1,128)} %bitcast.4), calls=%async_computation | async-start | bytes 8192 | tf_op jit(solution)/shard_map/all_to_all | solution.py:397
  10.3 10.0 %norm_rows.3.rest_1_.own = bf16[896,4096]{1,0:T(8,128)(2,1)} custom-call(bf16[1024,4096]{1,0:T(8,128)(2,1)} %rows.3, f32[4096]{0:T(1024)} %gain.3), custom_call_target="tpu_custom_call" | custom-call | tf_op jit(solution)/shard_map/norm_rows/pallas_call | solution.py:54
  24.5 7.8 %collective-permute-done.2 = s32[2,2,128]{2,1,0:T(2,128)S(1)} collective-permute-done((s32[2,2,128]{2,1,0:T(2,128)S(1)}, s32[2,2,128]{2,1,0:T(2,128)S(1)}, u32[]{:S(2)}, u32[]{:S(2)}) %collective-permute-start.2) | collective-permute-done | bytes 2080 | tf_op jit(solution)/shard_map/ppermute | solution.py:428
  32.9 1.5 collective-permute-start.3
  36.8 5.0 %pack_rows.3 = (bf16[192,4096]{1,0:T(8,128)(2,1)}, bf16[192,4096]{1,0:T(8,128)(2,1)S(1)}, bf16[128,4096]{1,0:T(8,128)(2,1)S(1)}, bf16[64,4096]{1,0:T(8,128)(2,1)S(1)}, bf16[64,4096]{1,0:T(8,128)(2,1)S(1)}) custom-call(s32[112]{0:T(128)S(1)} %select_reduce_fusion.3.listing, bf16[896,4096]{1,0:T(8,128)(2,1)} %norm_rows.3.rest_1_.own, ...), custom_call_target="tpu_custom_call" | custom-call | tf_op jit(solution)/shard_map/pack_rows/pallas_call | solution.py:107
  46.6 41.9 %block_acts.9 = f32[64,1664]{1,0:T(8,128)S(1)} custom-call(s32[384]{0:T(512)S(1)} %reshape.741.table, s32[256]{0:T(256)S(1)} %select_reduce_fusion.1.order, s32[5]{0:T(128)S(1)} %convert_reduce_fusion.10.bounds, bf16[128,4096]{1,0:T(8,128)(2,1)} %copy-done.2, bf16[896,4096]{1,0:T(8,128)(2,1)} %norm_rows.3.rest_1_.own, ...), custom_call_target="tpu_custom_call" | custom-call | flops 25769803776 | bytes 25165824 | tf_op jit(solution)/shard_map/block_acts/pallas_call | solution.py:268
  91.1 6.5 %all-to-all-start.2 = ((s32[8,1,128]{2,1,0:T(1,128)}), s32[8,1,128]{2,1,0:T(1,128)S(1)}, u32[]{:S(2)}, u32[]{:S(2)}) async-start(s32[8,1,128]{2,1,0:T(1,128)} %broadcast_in_dim.157), calls=%async_computation.2 | async-start | bytes 8192 | tf_op jit(solution)/shard_map/all_to_all | solution.py:448
  98.6 5.4 %all-to-all-done.2 = s32[8,1,128]{2,1,0:T(1,128)S(1)} async-done(((s32[8,1,128]{2,1,0:T(1,128)}), s32[8,1,128]{2,1,0:T(1,128)S(1)}, u32[]{:S(2)}, u32[]{:S(2)}) %all-to-all-start.2) | async-done | bytes 4128 | tf_op jit(solution)/shard_map/all_to_all | solution.py:448
  104.0 3.4 %all-to-all-start.1 = ((bf16[8,8,1664]{2,1,0:T(8,128)(2,1)}), bf16[8,8,1664]{2,1,0:T(8,128)(2,1)S(1)}, u32[]{:S(2)}, u32[]{:S(2)}) async-start(bf16[8,8,1664]{2,1,0:T(8,128)(2,1)} %convert_bitcast_fusion.1), calls=%async_computation.1 | async-start | bytes 425984 | tf_op jit(solution)/shard_map/all_to_all | solution.py:403
  108.8 6.5 %all-to-all-done.1 = bf16[8,8,1664]{2,1,0:T(8,128)(2,1)S(1)} async-done(((bf16[8,8,1664]{2,1,0:T(8,128)(2,1)}), bf16[8,8,1664]{2,1,0:T(8,128)(2,1)S(1)}, u32[]{:S(2)}, u32[]{:S(2)}) %all-to-all-start.1) | async-done | bytes 213024 | tf_op jit(solution)/shard_map/all_to_all | solution.py:403
  115.3 14.3 %block_acts.10 = f32[64,1664]{1,0:T(8,128)} custom-call(s32[384]{0:T(512)S(1)} %reshape.742.table, s32[32]{0:T(128)S(1)} %select_reduce_fusion.4.order, s32[3]{0:T(128)S(1)} %convert_reduce_fusion.11.bounds, bf16[128,4096]{1,0:T(8,128)(2,1)} %collective-permute-done.10.rest_0_, bf16[128,4096]{1,0:T(8,128)(2,1)} %collective-permute-done.11.rest_1_, ...), custom_call_target="tpu_custom_call" | custom-call | flops 3221225472 | bytes 25165824 | tf_op jit(solution)/shard_map/block_acts/pallas_call | solution.py:268
  129.7 4.6 %copy-done = bf16[4096,1536]{1,0:T(8,128)(2,1)S(1)} copy-done((bf16[4096,1536]{1,0:T(8,128)(2,1)S(1)}, bf16[4096,1536]{1,0:T(8,128)(2,1)}, u32[]{:S(2)}) %copy-start) | copy-done | bytes 12582936
  134.3 4.6 %copy-done.1 = bf16[4096,1536]{1,0:T(8,128)(2,1)S(1)} copy-done((bf16[4096,1536]{1,0:T(8,128)(2,1)S(1)}, bf16[4096,1536]{1,0:T(8,128)(2,1)}, u32[]{:S(2)}) %copy-start.1) | copy-done | bytes 12582936
  138.9 14.6 %block_acts.11.rest_4_ = f32[64,1664]{1,0:T(8,128)} custom-call(s32[384]{0:T(512)S(1)} %reshape.743.table, s32[256]{0:T(256)S(1)} %select_reduce_fusion.order, s32[7]{0:T(128)S(1)} %convert_reduce_fusion.9.bounds, bf16[192,4096]{1,0:T(8,128)(2,1)} %collective-permute-done.8.rest_0_, ...), custom_call_target="tpu_custom_call", output_to_operand_aliasing={{}: (7, {})} | custom-call | flops 4831838208 | bytes 25165824 | tf_op jit(solution)/shard_map/block_acts/pallas_call | solution.py:268
  154.1 1.6 collective-permute-start.16
  157.3 19.6 %block_acts.12.rest_4_ = f32[64,1664]{1,0:T(8,128)} custom-call(s32[384]{0:T(512)S(1)} %reshape.743.table, s32[256]{0:T(256)S(1)} %select_reduce_fusion.order, s32[7]{0:T(128)S(1)} %convert_reduce_fusion.9.bounds, bf16[192,4096]{1,0:T(8,128)(2,1)} %collective-permute-done.13.rest_0_, bf16[192,4096]{1,0:T(8,128)(2,1)} %copy-done.10, ...), custom_call_target="tpu_custom_call", output_to_operand_aliasing={{}: (7, {})} | custom-call | flops 4831838208 | bytes 25165824 | tf_op jit(solution)/shard_map/block_acts/pallas_call | solution.py:268
  178.1 14.1 %block_acts.13.rest_4_ = f32[64,1664]{1,0:T(8,128)} custom-call(s32[384]{0:T(512)S(1)} %reshape.743.table, s32[256]{0:T(256)S(1)} %select_reduce_fusion.order, s32[7]{0:T(128)S(1)} %convert_reduce_fusion.9.bounds, bf16[128,4096]{1,0:T(8,128)(2,1)} %collective-permute-done.7.rest_0_, bf16[128,4096]{1,0:T(8,128)(2,1)} %copy-done.11, ...), custom_call_target="tpu_custom_call", output_to_operand_aliasing={{}: (7, {})} | custom-call | flops 3221225472 | bytes 25165824 | tf_op jit(solution)/shard_map/block_acts/pallas_call | solution.py:268
  193.2 3.0 %block_acts.14.rest_4_ = f32[64,1664]{1,0:T(8,128)} custom-call(s32[384]{0:T(512)S(1)} %reshape.743.table, s32[256]{0:T(256)S(1)} %select_reduce_fusion.order, s32[7]{0:T(128)S(1)} %convert_reduce_fusion.9.bounds, bf16[64,4096]{1,0:T(8,128)(2,1)} %copy-done.13, bf16[64,4096]{1,0:T(8,128)(2,1)} %copy-done.14, ...), custom_call_target="tpu_custom_call", output_to_operand_aliasing={{}: (7, {})} | custom-call | flops 1610612736 | bytes 25165824 | tf_op jit(solution)/shard_map/block_acts/pallas_call | solution.py:268
  197.0 3.0 %block_acts.15 = f32[64,1664]{1,0:T(8,128)} custom-call(s32[384]{0:T(512)S(1)} %reshape.743.table, s32[256]{0:T(256)S(1)} %select_reduce_fusion.order, s32[7]{0:T(128)S(1)} %convert_reduce_fusion.9.bounds, bf16[64,4096]{1,0:T(8,128)(2,1)} %copy-done.12, bf16[64,4096]{1,0:T(8,128)(2,1)} %copy-done.15, ...), custom_call_target="tpu_custom_call", output_to_operand_aliasing={{}: (7, {})} | custom-call | flops 1610612736 | bytes 25165824 | tf_op jit(solution)/shard_map/block_acts/pallas_call | solution.py:268
  199.9 1.7 convert_bitcast_fusion
  201.6 17.3 %all-to-all-start.3 = ((bf16[8,8,1664]{2,1,0:T(8,128)(2,1)}), bf16[8,8,1664]{2,1,0:T(8,128)(2,1)S(1)}, u32[]{:S(2)}, u32[]{:S(2)}) async-start(bf16[8,8,1664]{2,1,0:T(8,128)(2,1)} %convert_bitcast_fusion), calls=%async_computation.3 | async-start | bytes 425984 | tf_op jit(solution)/shard_map/all_to_all | solution.py:403
  219.0 8.9 %all-to-all-done.3 = bf16[8,8,1664]{2,1,0:T(8,128)(2,1)S(1)} async-done(((bf16[8,8,1664]{2,1,0:T(8,128)(2,1)}), bf16[8,8,1664]{2,1,0:T(8,128)(2,1)S(1)}, u32[]{:S(2)}, u32[]{:S(2)}) %all-to-all-start.3) | async-done | bytes 213024 | tf_op jit(solution)/shard_map/all_to_all | solution.py:403
  227.9 2.1 collect_hits.1
  (166 shorter events, 22.1 us)
Async XLA Ops:
  2.5 17.8 %copy-start.2 = (bf16[128,4096]{1,0:T(8,128)(2,1)}, bf16[128,4096]{1,0:T(8,128)(2,1)S(1)}, u32[]{:S(2)}) copy-start(bf16[128,4096]{1,0:T(8,128)(2,1)S(1)} %norm_rows.2.rest_0_) | copy-start | bytes 3145732
  2.5 86.0 %collective-permute-start.10 = (bf16[128,4096]{1,0:T(8,128)(2,1)S(1)}, bf16[128,4096]{1,0:T(8,128)(2,1)}, u32[]{:S(2)}, u32[]{:S(2)}) collective-permute-start(bf16[128,4096]{1,0:T(8,128)(2,1)S(1)} %norm_rows.2.rest_0_), channel_id=1, source_target_pairs={{0,2},{1,3},{2,0},{3,1},{4,6},{5,7},{6,4},{7,5},{8,10},{9,11},{10,... | collective-permute-start | bytes 3145736 | tf_op jit(solution)/shard_map/ppermute | solution.py:375
  2.6 44.0 %collective-permute-start.4 = (bf16[128,4096]{1,0:T(8,128)(2,1)S(1)}, bf16[128,4096]{1,0:T(8,128)(2,1)}, u32[]{:S(2)}, u32[]{:S(2)}) collective-permute-start(bf16[128,4096]{1,0:T(8,128)(2,1)S(1)} %norm_rows.2.rest_0_), channel_id=1, source_target_pairs={{0,1},{1,0},{2,3},{3,2},{4,5},{5,4},{6,7},{7,6},{8,9},{9,8},{10,11... | collective-permute-start | bytes 3145736 | tf_op jit(solution)/shard_map/ppermute | solution.py:376
  4.0 17.0 %all-to-all-start = ((s32[8,1,64]{2,1,0:T(1,128)}), s32[8,1,64]{2,1,0:T(1,128)S(1)}, u32[]{:S(2)}, u32[]{:S(2)}) async-start(s32[8,1,64]{2,1,0:T(1,128)} %bitcast.4), calls=%async_computation | async-start | bytes 8192 | tf_op jit(solution)/shard_map/all_to_all | solution.py:397
  20.3 16.5 %collective-permute-start.5 = (bf16[896,4096]{1,0:T(8,128)(2,1)}, bf16[896,4096]{1,0:T(8,128)(2,1)}, u32[]{:S(2)}, u32[]{:S(2)}) collective-permute-start(bf16[896,4096]{1,0:T(8,128)(2,1)} %norm_rows.3.rest_1_.own), channel_id=1, source_target_pairs={{0,1},{1,0},{2,3},{3,2},{4,5},{5,4},{6,7},{7,6},{8,9},{9,8},{10,11... | collective-permute-start | bytes 22020104 | tf_op jit(solution)/shard_map/ppermute | solution.py:377
  22.4 9.9 %collective-permute-start.2 = (s32[2,2,128]{2,1,0:T(2,128)S(1)}, s32[2,2,128]{2,1,0:T(2,128)S(1)}, u32[]{:S(2)}, u32[]{:S(2)}) collective-permute-start(s32[2,2,128]{2,1,0:T(2,128)S(1)} %select_convert_fusion), channel_id=1, source_target_pairs={{0,1},{1,0},{2,3},{3,2},{4,5},{5,4},{6,7},{7,6},{8,9},{9,8},{10,11... | collective-permute-start | bytes 6152 | tf_op jit(solution)/shard_map/ppermute | solution.py:428
  32.9 3.6 %collective-permute-start.3 = (s32[2,128]{1,0:T(2,128)S(1)}, s32[2,128]{1,0:T(2,128)S(1)}, u32[]{:S(2)}, u32[]{:S(2)}) collective-permute-start(s32[2,128]{1,0:T(2,128)S(1)} %get-tuple-element.130), channel_id=1, source_target_pairs={{0,2},{1,3},{2,0},{3,1},{4,6},{5,7},{6,4},{7,5},{8,10},{9,11},{10,... | collective-permute-start | bytes 3080 | tf_op jit(solution)/shard_map/ppermute | solution.py:430
  44.6 53.0 %collective-permute-start.8 = (bf16[192,4096]{1,0:T(8,128)(2,1)}, bf16[192,4096]{1,0:T(8,128)(2,1)}, u32[]{:S(2)}, u32[]{:S(2)}) collective-permute-start(bf16[192,4096]{1,0:T(8,128)(2,1)} %get-tuple-element.69), channel_id=1, source_target_pairs={{0,2},{1,3},{2,0},{3,1},{4,6},{5,7},{6,4},{7,5},{8,10},{9,11},{10,... | collective-permute-start | bytes 4718600 | tf_op jit(solution)/shard_map/ppermute | solution.py:497
  45.8 83.8 %collective-permute-start.13 = (bf16[192,4096]{1,0:T(8,128)(2,1)S(1)}, bf16[192,4096]{1,0:T(8,128)(2,1)}, u32[]{:S(2)}, u32[]{:S(2)}) collective-permute-start(bf16[192,4096]{1,0:T(8,128)(2,1)S(1)} %get-tuple-element.78), channel_id=1, source_target_pairs={{0,2},{1,3},{2,0},{3,1},{4,6},{5,7},{6,4},{7,5},{8,10},{9,11},{10,... | collective-permute-start | bytes 4718600 | tf_op jit(solution)/shard_map/ppermute | solution.py:497
  88.5 26.8 %collective-permute-start.11 = (bf16[128,4096]{1,0:T(8,128)(2,1)}, bf16[128,4096]{1,0:T(8,128)(2,1)}, u32[]{:S(2)}, u32[]{:S(2)}) collective-permute-start(bf16[128,4096]{1,0:T(8,128)(2,1)} %collective-permute-done.10.rest_0_), channel_id=1, source_target_pairs={{0,1},{1,0},{2,3},{3,2},{4,5},{5,4},{6,7},{7,6},{8,9},{9,8},{10,11... | collective-permute-start | bytes 3145736 | tf_op jit(solution)/shard_map/ppermute | solution.py:515
  91.1 12.9 %all-to-all-start.2 = ((s32[8,1,128]{2,1,0:T(1,128)}), s32[8,1,128]{2,1,0:T(1,128)S(1)}, u32[]{:S(2)}, u32[]{:S(2)}) async-start(s32[8,1,128]{2,1,0:T(1,128)} %broadcast_in_dim.157), calls=%async_computation.2 | async-start | bytes 8192 | tf_op jit(solution)/shard_map/all_to_all | solution.py:448
  97.6 32.1 %collective-permute-start.9 = (bf16[192,4096]{1,0:T(8,128)(2,1)}, bf16[192,4096]{1,0:T(8,128)(2,1)}, u32[]{:S(2)}, u32[]{:S(2)}) collective-permute-start(bf16[192,4096]{1,0:T(8,128)(2,1)} %collective-permute-done.8.rest_0_), channel_id=1, source_target_pairs={{0,1},{1,0},{2,3},{3,2},{4,5},{5,4},{6,7},{7,6},{8,9},{9,8},{10,11... | collective-permute-start | bytes 4718600 | tf_op jit(solution)/shard_map/ppermute | solution.py:533
  104.0 11.2 %all-to-all-start.1 = ((bf16[8,8,1664]{2,1,0:T(8,128)(2,1)}), bf16[8,8,1664]{2,1,0:T(8,128)(2,1)S(1)}, u32[]{:S(2)}, u32[]{:S(2)}) async-start(bf16[8,8,1664]{2,1,0:T(8,128)(2,1)} %convert_bitcast_fusion.1), calls=%async_computation.1 | async-start | bytes 425984 | tf_op jit(solution)/shard_map/all_to_all | solution.py:403
  108.7 44.8 %collective-permute-start.7 = (bf16[128,4096]{1,0:T(8,128)(2,1)}, bf16[128,4096]{1,0:T(8,128)(2,1)}, u32[]{:S(2)}, u32[]{:S(2)}) collective-permute-start(bf16[128,4096]{1,0:T(8,128)(2,1)} %copy-done.3), channel_id=1, source_target_pairs={{0,2},{1,3},{2,0},{3,1},{4,6},{5,7},{6,4},{7,5},{8,10},{9,11},{10,... | collective-permute-start | bytes 3145736 | tf_op jit(solution)/shard_map/ppermute | solution.py:497
  129.5 24.6 %copy-start.7 = (bf16[64,4096]{1,0:T(8,128)(2,1)S(1)}, bf16[64,4096]{1,0:T(8,128)(2,1)}, u32[]{:S(2)}) copy-start(bf16[64,4096]{1,0:T(8,128)(2,1)} %copy-done.6) | copy-start | bytes 1572868
  129.6 26.2 %copy-start.5 = (bf16[64,4096]{1,0:T(8,128)(2,1)S(1)}, bf16[64,4096]{1,0:T(8,128)(2,1)}, u32[]{:S(2)}) copy-start(bf16[64,4096]{1,0:T(8,128)(2,1)} %copy-done.4) | copy-start | bytes 1572868
  129.6 26.6 %collective-permute-start.14 = (bf16[192,4096]{1,0:T(8,128)(2,1)}, bf16[192,4096]{1,0:T(8,128)(2,1)S(1)}, u32[]{:S(2)}, u32[]{:S(2)}) collective-permute-start(bf16[192,4096]{1,0:T(8,128)(2,1)} %collective-permute-done.13.rest_0_), channel_id=1, source_target_pairs={{0,1},{1,0},{2,3},{3,2},{4,5},{5,4},{6,7},{7,6},{8,9},{9,8},{10,11... | collective-permute-start | bytes 4718600 | tf_op jit(solution)/shard_map/ppermute | solution.py:533
  153.5 23.5 %collective-permute-start.12 = (bf16[128,4096]{1,0:T(8,128)(2,1)}, bf16[128,4096]{1,0:T(8,128)(2,1)S(1)}, u32[]{:S(2)}, u32[]{:S(2)}) collective-permute-start(bf16[128,4096]{1,0:T(8,128)(2,1)} %collective-permute-done.7.rest_0_), channel_id=1, source_target_pairs={{0,1},{1,0},{2,3},{3,2},{4,5},{5,4},{6,7},{7,6},{8,9},{9,8},{10,11... | collective-permute-start | bytes 3145736 | tf_op jit(solution)/shard_map/ppermute | solution.py:533
  154.1 22.8 %collective-permute-start.16 = (bf16[64,4096]{1,0:T(8,128)(2,1)S(1)}, bf16[64,4096]{1,0:T(8,128)(2,1)S(1)}, u32[]{:S(2)}, u32[]{:S(2)}) collective-permute-start(bf16[64,4096]{1,0:T(8,128)(2,1)S(1)} %copy-done.7), channel_id=1, source_target_pairs={{0,2},{1,3},{2,0},{3,1},{4,6},{5,7},{6,4},{7,5},{8,10},{9,11},{10,... | collective-permute-start | bytes 1572872 | tf_op jit(solution)/shard_map/ppermute | solution.py:497
  155.8 36.4 %collective-permute-start.6 = (bf16[64,4096]{1,0:T(8,128)(2,1)S(1)}, bf16[64,4096]{1,0:T(8,128)(2,1)S(1)}, u32[]{:S(2)}, u32[]{:S(2)}) collective-permute-start(bf16[64,4096]{1,0:T(8,128)(2,1)S(1)} %copy-done.5), channel_id=1, source_target_pairs={{0,2},{1,3},{2,0},{3,1},{4,6},{5,7},{6,4},{7,5},{8,10},{9,11},{10,... | collective-permute-start | bytes 1572872 | tf_op jit(solution)/shard_map/ppermute | solution.py:497
  176.9 15.3 %copy-start.13 = (bf16[64,4096]{1,0:T(8,128)(2,1)}, bf16[64,4096]{1,0:T(8,128)(2,1)S(1)}, u32[]{:S(2)}) copy-start(bf16[64,4096]{1,0:T(8,128)(2,1)S(1)} %collective-permute-done.16.rest_0_) | copy-start | bytes 1572868
  176.9 15.4 %collective-permute-start.17 = (bf16[64,4096]{1,0:T(8,128)(2,1)S(1)}, bf16[64,4096]{1,0:T(8,128)(2,1)S(1)}, u32[]{:S(2)}, u32[]{:S(2)}) collective-permute-start(bf16[64,4096]{1,0:T(8,128)(2,1)S(1)} %collective-permute-done.16.rest_0_), channel_id=1, source_target_pairs={{0,1},{1,0},{2,3},{3,2},{4,5},{5,4},{6,7},{7,6},{8,9},{9,8},{10,11... | collective-permute-start | bytes 1572872 | tf_op jit(solution)/shard_map/ppermute | solution.py:533
  192.2 4.0 %collective-permute-start.15 = (bf16[64,4096]{1,0:T(8,128)(2,1)S(1)}, bf16[64,4096]{1,0:T(8,128)(2,1)S(1)}, u32[]{:S(2)}, u32[]{:S(2)}) collective-permute-start(bf16[64,4096]{1,0:T(8,128)(2,1)S(1)} %collective-permute-done.6.rest_0_), channel_id=1, source_target_pairs={{0,1},{1,0},{2,3},{3,2},{4,5},{5,4},{6,7},{7,6},{8,9},{9,8},{10,11... | collective-permute-start | bytes 1572872 | tf_op jit(solution)/shard_map/ppermute | solution.py:533
  201.6 26.3 %all-to-all-start.3 = ((bf16[8,8,1664]{2,1,0:T(8,128)(2,1)}), bf16[8,8,1664]{2,1,0:T(8,128)(2,1)S(1)}, u32[]{:S(2)}, u32[]{:S(2)}) async-start(bf16[8,8,1664]{2,1,0:T(8,128)(2,1)} %convert_bitcast_fusion), calls=%async_computation.3 | async-start | bytes 425984 | tf_op jit(solution)/shard_map/all_to_all | solution.py:403
  (14 other events, 37.3 us)
